TPU v7x, 256 devices: a whole 4x4x8 slice. The times are simulated.
256 devices in a mesh: grp: 4 (over z_hi), freq: 64 (over z_lo, y, x, core).
Axes of the slice: x: 4, y: 4, z: 8 (z_hi: 4, z_lo: 2; z = z_hi * 2 + z_lo), core: 2. Of those that a mesh axis runs over, the one named last changes fastest.
Arguments:
- sources: bfloat16 [1024, 262144], P('freq', 'grp'), may hold values from -6 to 6
- panel_pos: float32 [3, 262144], P(None, 'grp'), may hold values from -1 to 1
- panel_blade: int32 [262144], P('grp'), may hold values from 0 to 3
- observer_table: float32 [3, 2048], replicated, may hold values from -8 to 8, as said below
- observer_index: int32 [32], replicated, may hold values from 0 to 2047
Outputs:
- spectra: float32 [512, 4, 2, 32], P('freq', 'grp')
Inputs may be any that keep to these rules, and one draw needn't show every extreme that they name: `observer_table`: each observer lies 3 to 8 units from the anchor (0, 0, 0).
All inputs are finite; a program needn't handle non-finite values.
Results may differ from a plain program's by a relative error of at most 0.0047.
Values may be sent and summed in bfloat16 or wider, within the bound.
No kernel may reach another device: no remote copies, remote signals or barrier semaphores. Data moves between devices by JAX's collectives and lax.ppermute only.
A program may use at most 64 MiB of HBM per device.

v0:
```python
import math

import jax
import jax.numpy as jnp
from jax import lax
from jax.sharding import PartitionSpec as P

NT = 1024
NF = 512
NCOMP = 4


wave_step = 0.04


def over_pieces(x, axis):
    return lax.all_gather(x, axis).sum(0)


def transform_table():
    row_index = jnp.arange(2 * NF, dtype=jnp.int32)
    samples = jnp.arange(NT, dtype=jnp.int32)
    frequency = row_index // 2
    parity = row_index % 2
    turn_count = frequency[:, None] * samples[None, :] % NT
    angle_table = 2.0 * math.pi / NT * turn_count.astype(jnp.float32)
    values = jnp.where(parity[:, None] == 0, jnp.cos(angle_table), -jnp.sin(angle_table))
    return (values / math.sqrt(NT)).astype(jnp.bfloat16)


def distances(positions, observers):
    offset_x = observers[0][:, None] - positions[0][None, :]
    offset_y = observers[1][:, None] - positions[1][None, :]
    offset_z = observers[2][:, None] - positions[2][None, :]
    return jnp.sqrt(offset_x * offset_x + offset_y * offset_y + offset_z * offset_z)


def blade_masks(blades):
    return (blades[None, :] == jnp.arange(NCOMP, dtype=jnp.int32)[:, None]).astype(jnp.bfloat16)


def frequency_term(frequency, spectrum_pair, blade_mask, distance, amplitude):
    wavenumber = wave_step * frequency.astype(jnp.float32)
    phase_angle = wavenumber * distance
    green_matrix = jnp.concatenate(
        [jnp.cos(phase_angle) * amplitude, -jnp.sin(phase_angle) * amplitude], axis=0
    ).astype(jnp.bfloat16)
    weighted = jnp.concatenate(
        [spectrum_pair[0][None, :] * blade_mask, spectrum_pair[1][None, :] * blade_mask], axis=0
    )
    product = lax.dot_general(
        weighted, green_matrix, (((1,), (1,)), ((), ())), preferred_element_type=jnp.float32
    )
    blade_count = blade_mask.shape[0]
    observer_count = distance.shape[0]
    real_part = product[:blade_count, :observer_count] - product[blade_count:, observer_count:]
    imag_part = product[:blade_count, observer_count:] + product[blade_count:, :observer_count]
    return jnp.stack([real_part, imag_part], axis=1)


def body(sources, panel_pos, panel_blade, observer_table, observer_index):
    freq_share = NF // lax.axis_size("freq")
    position = lax.axis_index("freq")
    observers = observer_table[:, observer_index]
    dft_table = transform_table()
    exchanged = lax.all_to_all(sources, "freq", split_axis=1, concat_axis=0, tiled=True)
    spectrum = jnp.dot(dft_table, exchanged, preferred_element_type=jnp.float32).astype(
        jnp.bfloat16
    )
    received = lax.all_to_all(spectrum, "freq", split_axis=0, concat_axis=1, tiled=True)
    spectra_pairs = received.reshape(freq_share, 2, received.shape[1])
    distance = distances(panel_pos, observers)
    amplitude = 0.25 / (math.pi * distance)
    blade_mask = blade_masks(panel_blade)
    frequencies = position * freq_share + jnp.arange(freq_share, dtype=jnp.int32)

    def per_frequency(element):
        return frequency_term(element[0], element[1], blade_mask, distance, amplitude)

    partial_value = lax.map(per_frequency, (frequencies, spectra_pairs))
    summed = over_pieces(partial_value, "grp")
    blade_share = NCOMP // lax.axis_size("grp")
    return lax.dynamic_slice_in_dim(summed, lax.axis_index("grp") * blade_share, blade_share, 1)


def solution(mesh):
    in_specs = (P("freq", "grp"), P(None, "grp"), P("grp"), P(), P())
    out_specs = P("freq", "grp", None, None)
    return jax.shard_map(body, mesh=mesh, in_specs=in_specs, out_specs=out_specs, check_vma=False)
```

profile of v0, /device:TPU:1, one launch (start us, length us, event | category | flops | bytes accessed | tf_op | source)
XLA Modules:
  0.0 449.2 jit_solution(7879830638706427243)
XLA Ops:
  0.0 3.2 copy.19
  3.2 10.3 %all-to-all-start = ((bf16[16,64,1024]{2,0,1:T(8,128)(2,1)}), bf16[16,64,1024]{2,0,1:T(8,128)(2,1)S(1)}, u32[]{:S(2)}, u32[]{:S(2)}) async-start(bf16[16,64,1024]{2,0,1:T(8,128)(2,1)} %bitcast.24), calls=%async_computation | async-start | bytes 4194304 | tf_op jit(solution)/shard_map/all_to_all | solution.py:66
  13.5 27.5 %all-to-all-done = bf16[16,64,1024]{2,0,1:T(8,128)(2,1)S(1)} async-done(((bf16[16,64,1024]{2,0,1:T(8,128)(2,1)}), bf16[16,64,1024]{2,0,1:T(8,128)(2,1)S(1)}, u32[]{:S(2)}, u32[]{:S(2)}) %all-to-all-start) | async-done | bytes 2097184 | tf_op jit(solution)/shard_map/all_to_all | solution.py:66
  41.1 21.4 %fusion.32 = bf16[1024,1024]{1,0:T(8,128)(2,1)} fusion(bf16[1024,1024]{1,0:T(8,128)(2,1)S(1)} %bitcast.34, s32[1024]{0:T(1024)S(1)} %add_select_fusion.1, pred[1024]{0:T(1024)(128)(4,1)S(1)} %fusion.33), kind=kOutput, calls=%fused_computation.45 | convolution fusion | flops 2167406592 | bytes 4199424 | tf_op jit(solution)/shard_map/dot_general | solution.py:67
  62.4 7.6 %all-to-all-start.1 = ((bf16[64,16,1024]{2,1,0:T(8,128)(2,1)}), bf16[64,16,1024]{2,1,0:T(8,128)(2,1)S(1)}, u32[]{:S(2)}, u32[]{:S(2)}) async-start(bf16[64,16,1024]{2,1,0:T(8,128)(2,1)} %bitcast.33), calls=%async_computation.1 | async-start | bytes 4194304 | tf_op jit(solution)/shard_map/all_to_all | solution.py:70
  70.1 1.4 fusion.44
  71.5 0.4 copy.15
  72.0 0.6 gather_fusion
  72.5 0.2 slice_reduce_fusion
  72.8 24.9 %all-to-all-done.1 = bf16[64,16,1024]{2,1,0:T(8,128)(2,1)S(1)} async-done(((bf16[64,16,1024]{2,1,0:T(8,128)(2,1)}), bf16[64,16,1024]{2,1,0:T(8,128)(2,1)S(1)}, u32[]{:S(2)}, u32[]{:S(2)}) %all-to-all-start.1) | async-done | bytes 2097184 | tf_op jit(solution)/shard_map/all_to_all | solution.py:70
  97.6 2.5 copy.14
  100.1 4.9 %reshape.45 = bf16[8,2,65536]{2,1,0:T(2,128)(2,1)S(1)} reshape(bf16[16,64,1024]{2,1,0:T(8,128)(2,1)} %copy.14) | data formatting | bytes 4194304 | tf_op jit(solution)/shard_map/reshape | solution.py:71
  105.0 0.0 copy-done
  105.1 329.8 %while.12 = (s32[]{:T(128)}, f32[8,4,2,32]{3,1,2,0:T(4,128)S(1)}, bf16[8,2,65536]{2,1,0:T(2,128)(2,1)S(1)}, s32[8]{0:T(128)S(1)}, s32[65536]{0:T(1024)S(1)}, /*i...) while((s32[]{:T(128)}, f32[8,4,2,32]{3,1,2,0:T(4,128)S(1)}, ...), condition=%wide.region_1.2_spmd.clone.clone, body=%wide.region_0.1_spmd.clone.clone.sunk | while | flops 120324608 | bytes 20723280 | solution.py:80
  105.1 0.6 dynamic_slice.18
  106.2 1.4 dynamic-slice_reduce_fusion.3
  107.6 0.5 fusion.53
  108.1 35.8 %multiply_convert_fusion.7 = (bf16[32,65536]{1,0:T(8,128)(2,1)S(1)}, bf16[32,65536]{1,0:T(8,128)(2,1)S(1)}) fusion(f32[65536]{0:T(1024)S(1)} %get-tuple-element.290, f32[32]{0:T(128)S(1)} %get-tuple-element.291, f32[65536]{0:T(1024)S(1)} %get-tuple-element.288, f32[32]{0:T(128)S(1)} %get-tuple-element.289, f32[65536]{0:T(1024)S(1)} %get-tuple-element.286, ...), kind=kLoop, calls=%fused_computation.11.clone.1 | loop fusion | flops 33554432 | bytes 9175428 | tf_op jit(solution)/shard_map/convert
  143.9 2.3 fusion.54
  146.2 0.1 subtract_bitcast_fusion.2
  146.3 0.6 dynamic_slice.18
  147.4 1.4 dynamic-slice_reduce_fusion.3
  148.9 0.5 fusion.53
  149.3 35.8 %multiply_convert_fusion.7 = (bf16[32,65536]{1,0:T(8,128)(2,1)S(1)}, bf16[32,65536]{1,0:T(8,128)(2,1)S(1)}) fusion(f32[65536]{0:T(1024)S(1)} %get-tuple-element.290, f32[32]{0:T(128)S(1)} %get-tuple-element.291, f32[65536]{0:T(1024)S(1)} %get-tuple-element.288, f32[32]{0:T(128)S(1)} %get-tuple-element.289, f32[65536]{0:T(1024)S(1)} %get-tuple-element.286, ...), kind=kLoop, calls=%fused_computation.11.clone.1 | loop fusion | flops 33554432 | bytes 9175428 | tf_op jit(solution)/shard_map/convert
  185.1 2.3 fusion.54
  187.4 0.1 subtract_bitcast_fusion.2
  187.5 0.6 dynamic_slice.18
  188.7 1.4 dynamic-slice_reduce_fusion.3
  190.1 0.5 fusion.53
  190.6 35.8 %multiply_convert_fusion.7 = (bf16[32,65536]{1,0:T(8,128)(2,1)S(1)}, bf16[32,65536]{1,0:T(8,128)(2,1)S(1)}) fusion(f32[65536]{0:T(1024)S(1)} %get-tuple-element.290, f32[32]{0:T(128)S(1)} %get-tuple-element.291, f32[65536]{0:T(1024)S(1)} %get-tuple-element.288, f32[32]{0:T(128)S(1)} %get-tuple-element.289, f32[65536]{0:T(1024)S(1)} %get-tuple-element.286, ...), kind=kLoop, calls=%fused_computation.11.clone.1 | loop fusion | flops 33554432 | bytes 9175428 | tf_op jit(solution)/shard_map/convert
  226.4 2.3 fusion.54
  228.6 0.1 subtract_bitcast_fusion.2
  228.7 0.6 dynamic_slice.18
  229.9 1.4 dynamic-slice_reduce_fusion.3
  231.3 0.5 fusion.53
  231.8 35.8 %multiply_convert_fusion.7 = (bf16[32,65536]{1,0:T(8,128)(2,1)S(1)}, bf16[32,65536]{1,0:T(8,128)(2,1)S(1)}) fusion(f32[65536]{0:T(1024)S(1)} %get-tuple-element.290, f32[32]{0:T(128)S(1)} %get-tuple-element.291, f32[65536]{0:T(1024)S(1)} %get-tuple-element.288, f32[32]{0:T(128)S(1)} %get-tuple-element.289, f32[65536]{0:T(1024)S(1)} %get-tuple-element.286, ...), kind=kLoop, calls=%fused_computation.11.clone.1 | loop fusion | flops 33554432 | bytes 9175428 | tf_op jit(solution)/shard_map/convert
  267.6 2.3 fusion.54
  269.8 0.1 subtract_bitcast_fusion.2
  269.9 0.6 dynamic_slice.18
  271.1 1.4 dynamic-slice_reduce_fusion.3
  272.5 0.5 fusion.53
  273.0 35.8 %multiply_convert_fusion.7 = (bf16[32,65536]{1,0:T(8,128)(2,1)S(1)}, bf16[32,65536]{1,0:T(8,128)(2,1)S(1)}) fusion(f32[65536]{0:T(1024)S(1)} %get-tuple-element.290, f32[32]{0:T(128)S(1)} %get-tuple-element.291, f32[65536]{0:T(1024)S(1)} %get-tuple-element.288, f32[32]{0:T(128)S(1)} %get-tuple-element.289, f32[65536]{0:T(1024)S(1)} %get-tuple-element.286, ...), kind=kLoop, calls=%fused_computation.11.clone.1 | loop fusion | flops 33554432 | bytes 9175428 | tf_op jit(solution)/shard_map/convert
  308.8 2.3 fusion.54
  311.1 0.1 subtract_bitcast_fusion.2
  311.2 0.6 dynamic_slice.18
  312.3 1.4 dynamic-slice_reduce_fusion.3
  313.7 0.5 fusion.53
  314.2 35.8 %multiply_convert_fusion.7 = (bf16[32,65536]{1,0:T(8,128)(2,1)S(1)}, bf16[32,65536]{1,0:T(8,128)(2,1)S(1)}) fusion(f32[65536]{0:T(1024)S(1)} %get-tuple-element.290, f32[32]{0:T(128)S(1)} %get-tuple-element.291, f32[65536]{0:T(1024)S(1)} %get-tuple-element.288, f32[32]{0:T(128)S(1)} %get-tuple-element.289, f32[65536]{0:T(1024)S(1)} %get-tuple-element.286, ...), kind=kLoop, calls=%fused_computation.11.clone.1 | loop fusion | flops 33554432 | bytes 9175428 | tf_op jit(solution)/shard_map/convert
  350.0 2.3 fusion.54
  352.3 0.1 subtract_bitcast_fusion.2
  352.4 0.6 dynamic_slice.18
  353.5 1.4 dynamic-slice_reduce_fusion.3
  355.0 0.5 fusion.53
  355.5 35.8 %multiply_convert_fusion.7 = (bf16[32,65536]{1,0:T(8,128)(2,1)S(1)}, bf16[32,65536]{1,0:T(8,128)(2,1)S(1)}) fusion(f32[65536]{0:T(1024)S(1)} %get-tuple-element.290, f32[32]{0:T(128)S(1)} %get-tuple-element.291, f32[65536]{0:T(1024)S(1)} %get-tuple-element.288, f32[32]{0:T(128)S(1)} %get-tuple-element.289, f32[65536]{0:T(1024)S(1)} %get-tuple-element.286, ...), kind=kLoop, calls=%fused_computation.11.clone.1 | loop fusion | flops 33554432 | bytes 9175428 | tf_op jit(solution)/shard_map/convert
  391.2 2.3 fusion.54
  393.5 0.1 subtract_bitcast_fusion.2
  393.6 0.6 dynamic_slice.18
  394.8 1.4 dynamic-slice_reduce_fusion.3
  396.2 0.5 fusion.53
  396.7 35.8 %multiply_convert_fusion.7 = (bf16[32,65536]{1,0:T(8,128)(2,1)S(1)}, bf16[32,65536]{1,0:T(8,128)(2,1)S(1)}) fusion(f32[65536]{0:T(1024)S(1)} %get-tuple-element.290, f32[32]{0:T(128)S(1)} %get-tuple-element.291, f32[65536]{0:T(1024)S(1)} %get-tuple-element.288, f32[32]{0:T(128)S(1)} %get-tuple-element.289, f32[65536]{0:T(1024)S(1)} %get-tuple-element.286, ...), kind=kLoop, calls=%fused_computation.11.clone.1 | loop fusion | flops 33554432 | bytes 9175428 | tf_op jit(solution)/shard_map/convert
  432.5 2.3 fusion.54
  434.7 0.1 subtract_bitcast_fusion.2
  434.8 13.7 %all-gather = f32[32,4,2,32]{3,1,2,0:T(4,128)S(1)} all-gather(f32[8,4,2,32]{3,1,2,0:T(4,128)S(1)} %get-tuple-element.42), channel_id=2, replica_groups=mesh['grp'=4,'freq'=64] {'grp'}, dimensions={0}, use_global_device_ids=true | all-gather | bytes 40960 | tf_op jit(solution)/shard_map/all_gather | solution.py:17
  448.5 0.6 constant_dynamic-slice_fusion
  (28 shorter events, 0.2 us)
Async XLA Ops:
  3.2 37.9 %all-to-all-start = ((bf16[16,64,1024]{2,0,1:T(8,128)(2,1)}), bf16[16,64,1024]{2,0,1:T(8,128)(2,1)S(1)}, u32[]{:S(2)}, u32[]{:S(2)}) async-start(bf16[16,64,1024]{2,0,1:T(8,128)(2,1)} %bitcast.24), calls=%async_computation | async-start | bytes 4194304 | tf_op jit(solution)/shard_map/all_to_all | solution.py:66
  62.4 7.7 %copy-start.1 = (f32[3,65536]{1,0:T(4,128)S(1)}, f32[3,65536]{1,0:T(4,128)}, u32[]{:S(2)}) copy-start(f32[3,65536]{1,0:T(4,128)} %param.8) | copy-start | bytes 2359300
  62.4 9.1 %copy-start.5 = (f32[3,2048]{1,0:T(4,128)S(1)}, f32[3,2048]{1,0:T(4,128)}, u32[]{:S(2)}) copy-start(f32[3,2048]{1,0:T(4,128)} %param.10) | copy-start | bytes 73732
  62.4 9.5 %copy-start.6 = (s32[32]{0:T(128)S(1)}, s32[32]{0:T(128)}, u32[]{:S(2)}) copy-start(s32[32]{0:T(128)} %param.11) | copy-start | bytes 388
  62.4 35.2 %all-to-all-start.1 = ((bf16[64,16,1024]{2,1,0:T(8,128)(2,1)}), bf16[64,16,1024]{2,1,0:T(8,128)(2,1)S(1)}, u32[]{:S(2)}, u32[]{:S(2)}) async-start(bf16[64,16,1024]{2,1,0:T(8,128)(2,1)} %bitcast.33), calls=%async_computation.1 | async-start | bytes 4194304 | tf_op jit(solution)/shard_map/all_to_all | solution.py:70
  97.6 7.4 %copy-start = (s32[65536]{0:T(1024)S(1)}, s32[65536]{0:T(1024)}, u32[]{:S(2)}) copy-start(s32[65536]{0:T(1024)} %param.9) | copy-start | bytes 786436
  97.6 7.4 %copy-start.2 = (f32[1,65536]{1,0:T(1,128)S(1)}, f32[1,65536]{1,0:T(1,128)}, u32[]{:S(2)}) copy-start(f32[1,65536]{1,0:T(1,128)} %get-tuple-element.165) | copy-start | bytes 786436
  97.6 7.4 %copy-start.3 = (f32[1,65536]{1,0:T(1,128)S(1)}, f32[1,65536]{1,0:T(1,128)}, u32[]{:S(2)}) copy-start(f32[1,65536]{1,0:T(1,128)} %get-tuple-element.166) | copy-start | bytes 786436
  97.6 7.4 %copy-start.4 = (f32[1,65536]{1,0:T(1,128)S(1)}, f32[1,65536]{1,0:T(1,128)}, u32[]{:S(2)}) copy-start(f32[1,65536]{1,0:T(1,128)} %get-tuple-element.167) | copy-start | bytes 786436
where the time goes:
time: 452 us; the launch traced here: 449 us
  other arithmetic  291 us (64%)
  waiting for transfers between devices  52.4 us (12%)
  matrix products  39.5 us (9%)
  local copies, waits for them, and re-layouts  29.8 us (7%)
  starting transfers between devices  18 us (4%)
  blocking collectives  13.7 us (3%)
  loops' own time  4.72 us (1%)
    another operation x8, other arithmetic  286 us
    all_to_all x1, waiting for transfers between devices, body(): lax.all_to_all(sources, 'freq', split_axis=1, concat_axis=0, tiled=True)  27.5 us
    all_to_all x1, waiting for transfers between devices, body(): lax.all_to_all(spectrum, 'freq', split_axis=0, concat_axis=1, tiled=True)  24.9 us
    dot_general x1, matrix products, body(): jnp.dot(dft_table, exchanged, preferred_element_type=jnp.float32)  21.4 us
    dot_general x8, matrix products, frequency_term(): lax.dot_general(weighted, green_matrix, (((1,), (1,)), ((), ())), preferr...  18.1 us
    all_gather x1, blocking collectives, over_pieces(): return lax.all_gather(x, axis).sum(0)  13.7 us
    slice x8, local copies, waits for them, and re-layouts, frequency_term(): spectrum_pair[0][None, :] * blade_mask  11.3 us
    all_to_all x1, starting transfers between devices, body(): lax.all_to_all(sources, 'freq', split_axis=1, concat_axis=0, tiled=True)  10.3 us
  transfers between devices with their start and end apart: 2, of which 2 were waited for; matrix products, arithmetic and copies ran while one was open for 1% of the time, Pallas kernels for 0%

commit v1 on v0

v1 whole, which is shorter than its diff:
```python
import functools
import math

import jax
import jax.numpy as jnp
from jax import lax
from jax.experimental import pallas as pl
from jax.experimental.pallas import tpu as pltpu
from jax.sharding import PartitionSpec as P

NT = 1024
NF = 512
NCOMP = 4
QUAD = 4
BLOCK = 4
F32, BF16 = jnp.float32, jnp.bfloat16

wave_step = 0.04


def transform_table():
    samples = jnp.arange(NT, dtype=jnp.int32)
    small = jnp.arange(32, dtype=jnp.int32)
    turn = 2.0 * math.pi / NT
    low = turn * (small[:, None] * samples[None, :] % NT).astype(F32)
    high = turn * (32 * small[: NF // 32, None] * samples[None, :] % NT).astype(F32)
    cl, sl = jnp.cos(low), jnp.sin(low)
    scale = 1.0 / math.sqrt(NT)
    ch, sh = jnp.cos(high) * scale, jnp.sin(high) * scale
    cl, sl, ch, sh = lax.optimization_barrier((cl, sl, ch, sh))
    re = ch[:, None] * cl[None] - sh[:, None] * sl[None]
    im = -(sh[:, None] * cl[None] + ch[:, None] * sl[None])
    return jnp.stack([re, im], axis=2).reshape(2 * NF, NT).astype(BF16)


def green_start(positions, observers):
    columns = positions.T
    lane_observers = jnp.tile(observers, (1, QUAD))
    offset_x = lane_observers[0][None, :] - columns[:, 0:1]
    offset_y = lane_observers[1][None, :] - columns[:, 1:2]
    offset_z = lane_observers[2][None, :] - columns[:, 2:3]
    distance = jnp.sqrt(offset_x * offset_x + offset_y * offset_y + offset_z * offset_z)
    amplitude = 0.25 / (math.pi * distance)
    offset = jnp.repeat(jnp.arange(QUAD, dtype=F32), observers.shape[1])
    near = (wave_step * (offset - QUAD))[None, :] * distance
    far = (wave_step * (offset - 2 * QUAD))[None, :] * distance
    turn = 2.0 * jnp.cos((wave_step * QUAD) * distance)
    return (
        turn,
        jnp.cos(near) * amplitude,
        -jnp.sin(near) * amplitude,
        jnp.cos(far) * amplitude,
        -jnp.sin(far) * amplitude,
    )


def radiate_kernel(
    table_ref, source_ref, turn_ref, c1_ref, s1_ref, c2_ref, s2_ref, blade_ref, out_ref,
    spectrum, masks, ca, sa, cb, sb, green_a, green_b,
):
    panels = source_ref.shape[1]
    quads = NF // QUAD
    spectrum[...] = jnp.dot(table_ref[...], source_ref[...], preferred_element_type=F32).astype(BF16)
    for b in range(NCOMP):
        masks[b] = jnp.broadcast_to(
            jnp.where(blade_ref[...] == b, 1.0, 0.0), (16, panels)
        ).astype(BF16)
    ca[...] = c1_ref[...]
    sa[...] = s1_ref[...]
    cb[...] = c2_ref[...]
    sb[...] = s2_ref[...]
    row = lax.broadcasted_iota(jnp.int32, (8, 128), 0)
    lane = lax.broadcasted_iota(jnp.int32, (8, 128), 1)
    diagonal = (row // 2) == (lane // 32)
    even = (row % 2) == 0

    def generate(green):
        for chunk in range(panels // 16):
            rows = pl.ds(16 * chunk, 16)
            turn = turn_ref[rows, :]
            c, s, cp, sp = ca[rows, :], sa[rows, :], cb[rows, :], sb[rows, :]
            for k in range(BLOCK):
                c, cp = turn * c - cp, c
                s, sp = turn * s - sp, s
                green[k, rows, 0:128] = c.astype(BF16)
                green[k, rows, 128:256] = s.astype(BF16)
            ca[rows, :] = c
            sa[rows, :] = s
            cb[rows, :] = cp
            sb[rows, :] = sp

    def contract(block, green):
        for pair in range(BLOCK // 2):
            start = block * (BLOCK * 8) + pair * 16
            part = spectrum[pl.ds(pl.multiple_of(start, 16), 16), :]
            weighted = jnp.concatenate([part * masks[b] for b in range(NCOMP)], axis=0)
            for k2 in range(2):
                k = pair * 2 + k2
                r = jnp.dot(weighted, green[k], preferred_element_type=F32)
                acc_re = None
                for b in range(NCOMP):
                    top = 16 * b + 8 * k2
                    u = r[top : top + 8, 0:128]
                    v = r[top : top + 8, 128:256]
                    w = jnp.where(even, -pltpu.roll(v, 7, 0), pltpu.roll(v, 1, 0))
                    z = jnp.where(diagonal, u + w, 0.0)
                    if b:
                        z = pltpu.roll(z, 2 * b, 0)
                    acc_re = z if acc_re is None else acc_re + z
                y = acc_re
                for j in range(1, QUAD):
                    y = jnp.where(lane // 32 == j, pltpu.roll(acc_re, 8 - 2 * j, 0), y)
                out_ref[block * BLOCK + k] = y

    generate(green_a)

    def step(i, carry):
        generate(green_b)
        contract(2 * i, green_a)
        generate(green_a)
        contract(2 * i + 1, green_b)
        return carry

    lax.fori_loop(0, quads // BLOCK // 2, step, 0)


def radiate(table, exchanged, start, blades, interpret=False):
    panels = exchanged.shape[1]
    quads = NF // QUAD
    vm = pl.BlockSpec(memory_space=pltpu.VMEM)
    state = pltpu.VMEM((panels, 128), F32)
    return pl.pallas_call(
        radiate_kernel,
        out_shape=jax.ShapeDtypeStruct((quads, 8, 128), F32),
        in_specs=[vm] * 8,
        out_specs=vm,
        scratch_shapes=[
            pltpu.VMEM((2 * NF, panels), BF16),
            pltpu.VMEM((NCOMP, 16, panels), BF16),
            state, state, state, state,
            pltpu.VMEM((BLOCK, panels, 256), BF16),
            pltpu.VMEM((BLOCK, panels, 256), BF16),
        ],
        compiler_params=pltpu.CompilerParams(vmem_limit_bytes=48 * 1024 * 1024),
        cost_estimate=pl.CostEstimate(flops=20_000_000_000, bytes_accessed=8_000_000, transcendentals=0),
        name="radiate",
    )(table, exchanged, *start, blades[None, :])


def body(sources, panel_pos, panel_blade, observer_table, observer_index):
    width = sources.shape[1] // lax.axis_size("freq")
    position = lax.axis_index("freq")
    observers = observer_table[:, observer_index]
    exchanged = lax.all_to_all(sources, "freq", split_axis=1, concat_axis=0, tiled=True)
    table = transform_table()
    own_pos = lax.dynamic_slice_in_dim(panel_pos, position * width, width, 1)
    own_blade = lax.dynamic_slice_in_dim(panel_blade, position * width, width, 0)
    start = green_start(own_pos, observers)
    partial = radiate(table, exchanged, start, own_blade)
    owners = lax.axis_size("freq")
    blocks = partial.reshape(owners, NF // QUAD // owners, NCOMP, 2, 128)
    blocks = blocks.transpose(0, 2, 1, 3, 4).astype(BF16)
    blocks = blocks.reshape(owners * NCOMP, -1, 128)
    arrived = lax.all_to_all(blocks, ("freq", "grp"), split_axis=0, concat_axis=0, tiled=True)
    total = arrived.astype(F32).sum(0)
    total = total.reshape(-1, 2, QUAD, observers.shape[1]).transpose(0, 2, 1, 3)
    return total.reshape(NF // owners, 1, 2, observers.shape[1])


def solution(mesh):
    in_specs = (P("freq", "grp"), P(None, "grp"), P("grp"), P(), P())
    out_specs = P("freq", "grp", None, None)
    return jax.shard_map(body, mesh=mesh, in_specs=in_specs, out_specs=out_specs, check_vma=False)
```

time: 452 us -> 102 us (0.23)
  other arithmetic: 291 us -> 19.1 us
  waiting for transfers between devices: 52.4 us -> 1.38 us
  matrix products: 39.5 us -> 0 us
  Pallas kernels: 0 us -> 25.5 us
  blocking collectives: 13.7 us -> 28.3 us
  local copies, waits for them, and re-layouts: 29.8 us -> 16.6 us
  starting transfers between devices: 18 us -> 10.5 us
  loops' own time: 4.72 us -> 0 us
    another operation x16 -> x2, other arithmetic: 287 us -> 10.1 us  [the longest x1 5.21 us: transform_table(): return jnp.stack([re, im], axis=2).reshape(2 * NF, NT).astype(BF16)]
    dot_general x9 -> x0, matrix products: 39.5 us -> none  [the longest x1 21.4 us: body(): jnp.dot(dft_table, exchanged, preferred_element_type=jnp.float32)]
    all_to_all x0 -> x1, blocking collectives: none -> 28.3 us  [body(): lax.all_to_all(blocks, ('freq', 'grp'), split_axis=0, concat_axis=0, tile...]
    all_to_all x1, waiting for transfers between devices: 27.5 us -> 1.38 us  [body(): lax.all_to_all(sources, 'freq', split_axis=1, concat_axis=0, tiled=True)]
    pallas_call x0 -> x1, Pallas kernels: none -> 25.5 us  [radiate(): pl.pallas_call(radiate_kernel, out_shape=jax.ShapeDtypeStruct((quads, 8,...]
    all_to_all x1 -> x0, waiting for transfers between devices: 24.9 us -> none  [body(): lax.all_to_all(spectrum, 'freq', split_axis=0, concat_axis=1, tiled=True)]
    all_gather x1 -> x0, blocking collectives: 13.7 us -> none  [over_pieces(): return lax.all_gather(x, axis).sum(0)]
    slice x10 -> x2, local copies, waits for them, and re-layouts: 13 us -> 0.19 us  [green_start(): offset_x = lane_observers[0][None, :] - columns[:, 0:1]]
  transfers between devices with their start and end apart: 2 -> 1, of which waited for: 2 -> 1; matrix products, arithmetic and copies ran while one was open for 1% -> 26% of each run, Pallas kernels for 0% -> 0%
where the time goes in v1:
time: 102 us
  blocking collectives  28.3 us (28%)
  Pallas kernels  25.5 us (25%)
  other arithmetic  19.1 us (19%)
  local copies, waits for them, and re-layouts  16.6 us (16%)
  starting transfers between devices  10.5 us (10%)
  waiting for transfers between devices  1.38 us (1%)
    all_to_all x1, blocking collectives, body(): lax.all_to_all(blocks, ('freq', 'grp'), split_axis=0, concat_axis=0, tile...  28.3 us
    pallas_call x1, Pallas kernels, radiate(): pl.pallas_call(radiate_kernel, out_shape=jax.ShapeDtypeStruct((quads, 8,...  25.5 us
    all_to_all x1, starting transfers between devices, body(): lax.all_to_all(sources, 'freq', split_axis=1, concat_axis=0, tiled=True)  10.5 us
    mul x1, other arithmetic, green_start(): -jnp.sin(far) * amplitude  7.71 us
    unnamed x17, local copies, waits for them, and re-layouts  6.57 us
    another operation x1, other arithmetic, transform_table(): return jnp.stack([re, im], axis=2).reshape(2 * NF, NT).astype(BF16)  5.21 us
    another operation x1, other arithmetic  4.94 us
    all_to_all x1, local copies, waits for them, and re-layouts, body(): lax.all_to_all(sources, 'freq', split_axis=1, concat_axis=0, tiled=True)  3.23 us
  transfers between devices with their start and end apart: 1, of which 1 were waited for; matrix products, arithmetic and copies ran while one was open for 26% of the time, Pallas kernels for 0%

profile of v1, /device:TPU:1, one launch (start us, length us, event | category | flops | bytes accessed | tf_op | source)
XLA Modules:
  0.0 101.6 jit_solution(14484882070500293296)
XLA Ops:
  0.0 0.0 copy-start
  0.0 3.2 %copy.24 = bf16[2,64,8,1024]{3,2,0,1:T(8,128)(2,1)} copy(bf16[2,64,8,1024]{3,2,1,0:T(8,128)(2,1)} %bitcast.21) | data formatting | bytes 4194304 | tf_op jit(solution)/shard_map/all_to_all | solution.py:154
  3.2 10.5 %all-to-all-start = ((bf16[16,64,1024]{2,0,1:T(8,128)(2,1)}), bf16[16,64,1024]{2,0,1:T(8,128)(2,1)}, u32[]{:S(2)}, u32[]{:S(2)}) async-start(bf16[16,64,1024]{2,0,1:T(8,128)(2,1)} %bitcast.19), calls=%async_computation | async-start | bytes 4194304 | tf_op jit(solution)/shard_map/all_to_all | solution.py:154
  13.8 0.5 fusion.11
  14.3 0.3 sine_multiply_fusion
  14.7 4.9 %subtract_convert_fusion = (bf16[16,32,1,1024]{3,2,1,0:T(2,128)(2,1)S(1)}, bf16[16,32,1,1024]{3,2,1,0:T(2,128)(2,1)S(1)}) fusion(f32[32,1024]{1,0:T(8,128)S(1)} %get-tuple-element.12, f32[16,1024]{1,0:T(8,128)S(1)} %get-tuple-element.11, f32[32,1024]{1,0:T(8,128)S(1)} %get-tuple-element.10, f32[16,1024]{1,0:T(8,128)S(1)} %get-tuple-element.9), kind=kLoop, calls=%fused_computation.4 | loop fusion | flops 4718592 | bytes 2490368 | tf_op jit(solution)/shard_map/convert
  19.6 5.2 %pad_maximum_fusion = bf16[16,32,2,1024]{3,2,1,0:T(2,128)(2,1)} fusion(bf16[16,32,1,1024]{3,2,1,0:T(2,128)(2,1)S(1)} %get-tuple-element.17, bf16[16,32,1,1024]{3,2,1,0:T(2,128)(2,1)S(1)} %get-tuple-element.16), kind=kLoop, calls=%fused_computation.2 | loop fusion | flops 4194304 | bytes 4194304 | tf_op jit(solution)/shard_map/stack | solution.py:33
  24.8 0.0 copy-start.6
  24.8 0.0 copy-start.7
  24.8 2.8 %convert_element_type.27.table_ref = bf16[1024,1024]{1,0:T(8,128)(2,1)S(1)} reshape(bf16[16,32,2,1024]{3,2,1,0:T(2,128)(2,1)} %pad_maximum_fusion) | data formatting | bytes 4194304 | tf_op jit(solution)/shard_map/convert_element_type | solution.py:33
  27.6 0.1 mul.255
  27.7 0.0 copy-done.6
  27.7 1.4 %copy.17 = f32[3,2048]{0,1:T(8,128)} copy(f32[3,2048]{1,0:T(4,128)S(1)} %copy-done.6) | data formatting | bytes 49152 | tf_op args[3]
  29.0 0.0 copy-done.7
  29.1 1.8 %gather_fusion = f32[32,3]{1,0:T(8,128)S(1)} fusion(f32[3,2048]{0,1:T(8,128)} %copy.17, s32[1024]{0:T(1024)S(1)} %pad_clamp_fusion), kind=kCustom, calls=%fused_computation | custom fusion | bytes 896 | tf_op jit(solution)/shard_map/gather | solution.py:153
  30.9 0.2 slice_reduce_fusion.2
  31.0 0.1 tile.22
  31.1 0.1 tile.20
  31.2 0.1 tile.18
  31.3 0.1 mul.247
  31.4 0.7 dynamic_slice.7
  32.1 0.0 copy-done
  32.1 7.7 %negate_multiply_fusion = (f32[1024,128]{1,0:T(8,128)}, f32[1024,128]{1,0:T(8,128)}, f32[1024,128]{1,0:T(8,128)}, f32[1024,128]{1,0:T(8,128)}, f32[1024,128]{1,0:T(8,128)}) fusion(f32[128]{0:T(128)S(1)} %mul.255, f32[1024]{0:T(1024)S(1)} %bitcast.28, f32[128]{0:T(128)S(1)} %tile.22, f32[1024]{0:T(1024)S(1)} %bitcast.29, f32[128]{0:T(128)S(1)} %tile.20, ...), kind=kLoop, calls=%fused_computation.6 | loop fusion | flops 2621440 | bytes 2636288 | tf_op jit(solution)/shard_map/mul | solution.py:53
  39.8 1.4 %all-to-all-done = bf16[16,64,1024]{2,0,1:T(8,128)(2,1)} async-done(((bf16[16,64,1024]{2,0,1:T(8,128)(2,1)}), bf16[16,64,1024]{2,0,1:T(8,128)(2,1)}, u32[]{:S(2)}, u32[]{:S(2)}) %all-to-all-start) | async-done | bytes 2097184 | tf_op jit(solution)/shard_map/all_to_all | solution.py:154
  41.2 0.0 copy-start.1
  41.2 1.0 %copy-done.1 = f32[1024,128]{1,0:T(8,128)S(1)} copy-done((f32[1024,128]{1,0:T(8,128)S(1)}, f32[1024,128]{1,0:T(8,128)}, u32[]{:S(2)}) %copy-start.1) | copy-done | bytes 524312
  42.3 0.0 copy-start.2
  42.3 1.0 %copy-done.2 = f32[1024,128]{1,0:T(8,128)S(1)} copy-done((f32[1024,128]{1,0:T(8,128)S(1)}, f32[1024,128]{1,0:T(8,128)}, u32[]{:S(2)}) %copy-start.2) | copy-done | bytes 524312
  43.3 0.0 copy-start.3
  43.3 1.0 %copy-done.3 = f32[1024,128]{1,0:T(8,128)S(1)} copy-done((f32[1024,128]{1,0:T(8,128)S(1)}, f32[1024,128]{1,0:T(8,128)}, u32[]{:S(2)}) %copy-start.3) | copy-done | bytes 524312
  44.3 0.0 copy-start.4
  44.3 1.0 %copy-done.4 = f32[1024,128]{1,0:T(8,128)S(1)} copy-done((f32[1024,128]{1,0:T(8,128)S(1)}, f32[1024,128]{1,0:T(8,128)}, u32[]{:S(2)}) %copy-start.4) | copy-done | bytes 524312
  45.4 0.0 copy-start.5
  45.4 1.0 %copy-done.5 = f32[1024,128]{1,0:T(8,128)S(1)} copy-done((f32[1024,128]{1,0:T(8,128)S(1)}, f32[1024,128]{1,0:T(8,128)}, u32[]{:S(2)}) %copy-start.5) | copy-done | bytes 524312
  46.4 25.5 %radiate.1 = f32[128,8,128]{2,1,0:T(8,128)S(1)} custom-call(bf16[1024,1024]{1,0:T(8,128)(2,1)S(1)} %convert_element_type.27.table_ref, bf16[1024,1024]{1,0:T(8,128)(2,1)} %bitcast.1.source_ref, f32[1024,128]{1,0:T(8,128)S(1)} %copy-done.5, f32[1024,128]{1,0:T(8,128)S(1)} %copy-done.3, f32[1024,128]{1,0:T(8,128)S(1)} %copy-done.4, f32[1024,128]{1,0:T(8,128)S(1)} %copy-done.2, ...), custom_call_target="tpu_custom_call" | custom-call | flops 20000000000 | bytes 8000000 | tf_op jit(solution)/shard_map/radiate/pallas_call | solution.py:132
  72.0 0.1 copy.18
  72.1 0.2 copy.19
  72.3 28.3 %all_to_all.24 = bf16[256,4,128]{2,1,0:T(4,128)(2,1)S(1)} all-to-all(bf16[256,4,128]{2,1,0:T(4,128)(2,1)S(1)} %copy.19), channel_id=1, replica_groups=mesh['grp'=4,'freq'=64] {'freq','grp'}, dimensions={0} | all-to-all | bytes 524288 | tf_op jit(solution)/shard_map/all_to_all | solution.py:164
  100.6 0.3 convert_reduce_fusion
  100.9 0.1 reshape.80
  101.0 0.6 copy.21
  (13 shorter events, 0.1 us)
Async XLA Ops:
  0.0 32.1 %copy-start = (f32[3,65536]{1,0:T(4,128)S(1)}, f32[3,65536]{1,0:T(4,128)}, u32[]{:S(2)}) copy-start(f32[3,65536]{1,0:T(4,128)} %param.6) | copy-start | bytes 2359300
  3.2 38.0 %all-to-all-start = ((bf16[16,64,1024]{2,0,1:T(8,128)(2,1)}), bf16[16,64,1024]{2,0,1:T(8,128)(2,1)}, u32[]{:S(2)}, u32[]{:S(2)}) async-start(bf16[16,64,1024]{2,0,1:T(8,128)(2,1)} %bitcast.19), calls=%async_computation | async-start | bytes 4194304 | tf_op jit(solution)/shard_map/all_to_all | solution.py:154
  24.8 2.9 %copy-start.6 = (f32[3,2048]{1,0:T(4,128)S(1)}, f32[3,2048]{1,0:T(4,128)}, u32[]{:S(2)}) copy-start(f32[3,2048]{1,0:T(4,128)} %param.8) | copy-start | bytes 73732
  24.8 4.2 %copy-start.7 = (s32[32]{0:T(128)S(1)}, s32[32]{0:T(128)}, u32[]{:S(2)}) copy-start(s32[32]{0:T(128)} %param.9) | copy-start | bytes 388
  41.2 1.0 %copy-start.1 = (f32[1024,128]{1,0:T(8,128)S(1)}, f32[1024,128]{1,0:T(8,128)}, u32[]{:S(2)}) copy-start(f32[1024,128]{1,0:T(8,128)} %get-tuple-element.21.s2_ref) | copy-start | bytes 1572868
  42.3 1.0 %copy-start.2 = (f32[1024,128]{1,0:T(8,128)S(1)}, f32[1024,128]{1,0:T(8,128)}, u32[]{:S(2)}) copy-start(f32[1024,128]{1,0:T(8,128)} %get-tuple-element.22.c2_ref) | copy-start | bytes 1572868
  43.3 1.0 %copy-start.3 = (f32[1024,128]{1,0:T(8,128)S(1)}, f32[1024,128]{1,0:T(8,128)}, u32[]{:S(2)}) copy-start(f32[1024,128]{1,0:T(8,128)} %get-tuple-element.25.c1_ref) | copy-start | bytes 1572868
  44.3 1.0 %copy-start.4 = (f32[1024,128]{1,0:T(8,128)S(1)}, f32[1024,128]{1,0:T(8,128)}, u32[]{:S(2)}) copy-start(f32[1024,128]{1,0:T(8,128)} %get-tuple-element.26.s1_ref) | copy-start | bytes 1572868
  45.4 1.0 %copy-start.5 = (f32[1024,128]{1,0:T(8,128)S(1)}, f32[1024,128]{1,0:T(8,128)}, u32[]{:S(2)}) copy-start(f32[1024,128]{1,0:T(8,128)} %get-tuple-element.27.turn_ref) | copy-start | bytes 1572868

commit v2 on v0

v2 whole, which is shorter than its diff:
```python
import functools
import math

import jax
import jax.numpy as jnp
from jax import lax
from jax.experimental import pallas as pl
from jax.experimental.pallas import tpu as pltpu
from jax.sharding import PartitionSpec as P

NT = 1024
NF = 512
NCOMP = 4
QUAD = 4
BLOCK = 16
STREAMS = 2
GROUP = 2
POP = 1
F32, BF16 = jnp.float32, jnp.bfloat16

wave_step = 0.04


def transform_table():
    samples = jnp.arange(NT, dtype=jnp.int32)
    low_row = jnp.arange(64, dtype=jnp.int32)
    high_row = jnp.arange(NF // 32, dtype=jnp.int32)
    turn = 2.0 * math.pi / NT
    low_count = ((low_row // 2)[:, None] * samples[None, :] + (NT // 4) * (low_row % 2)[:, None]) % NT
    high_count = 32 * high_row[:, None] * samples[None, :] % NT
    low = turn * low_count.astype(F32)
    high = turn * high_count.astype(F32)
    scale = 1.0 / math.sqrt(NT)
    cl, sl = jnp.cos(low), jnp.sin(low)
    ch, sh = jnp.cos(high) * scale, jnp.sin(high) * scale
    cl, sl, ch, sh = lax.optimization_barrier((cl, sl, ch, sh))
    rows = ch[:, None] * cl[None] - sh[:, None] * sl[None]
    return rows.astype(BF16).reshape(2 * NF, NT)


def prepare_kernel(column_ref, observer_ref, out_ref):
    offset = (lax.broadcasted_iota(jnp.int32, (16, 128), 1) // 32 - QUAD).astype(F32) * wave_step
    observers = [jnp.broadcast_to(observer_ref[i : i + 1, :], (16, 128)) for i in range(3)]

    def cos_sin(x):
        x2 = x * x
        c, s = 1.0 / math.factorial(14), 1.0 / math.factorial(15)
        c, s = -c, -s
        for n in range(6, -1, -1):
            sign = 1.0 if n % 2 == 0 else -1.0
            c = c * x2 + sign / math.factorial(2 * n)
            s = s * x2 + sign / math.factorial(2 * n + 1)
        return c, s * x

    def step(i, carry):
        rows = pl.ds(pl.multiple_of(16 * i, 16), 16)
        square = None
        for axis in range(3):
            diff = observers[axis] - column_ref[rows, axis : axis + 1]
            square = diff * diff if square is None else square + diff * diff
        distance = jnp.sqrt(square)
        amplitude = 0.25 / (math.pi * distance)
        cn, sn = cos_sin(offset * distance)
        cq, sq = cos_sin((wave_step * QUAD) * distance)
        c1, s1 = cn * amplitude, -sn * amplitude
        out_ref[0, rows, :] = 2.0 * cq
        out_ref[1, rows, :] = c1
        out_ref[2, rows, :] = s1
        out_ref[3, rows, :] = c1 * cq - s1 * sq
        out_ref[4, rows, :] = s1 * cq + c1 * sq
        return carry

    lax.fori_loop(0, out_ref.shape[1] // 16, step, 0)


def green_start(positions, observers):
    panels = positions.shape[1]
    vm = pl.BlockSpec(memory_space=pltpu.VMEM)
    return pl.pallas_call(
        prepare_kernel,
        out_shape=jax.ShapeDtypeStruct((5, panels, 128), F32),
        in_specs=[vm, vm],
        out_specs=vm,
        compiler_params=pltpu.CompilerParams(vmem_limit_bytes=8 * 1024 * 1024),
        cost_estimate=pl.CostEstimate(flops=20_000_000, bytes_accessed=3_000_000, transcendentals=0),
        name="prepare",
    )(positions.T, jnp.tile(observers, (1, QUAD)))


def radiate_kernel(
    zero_ref, table_hbm, source_hbm, start_ref, blade_ref, out_ref,
    table_ref, source_ref, spectrum, masks, weighted, green_a, green_b, sems, *states
):
    panels = source_ref.shape[1]
    share = panels // STREAMS
    blocks = NF // QUAD // BLOCK
    tiles = panels // 256
    pairs = BLOCK // 2
    chunks = panels // 16
    row = lax.broadcasted_iota(jnp.int32, (8, 128), 0)
    lane = lax.broadcasted_iota(jnp.int32, (8, 128), 1)
    diagonal = (row // 2) == (lane // 32)
    even = (row % 2) == 0
    zero = zero_ref[0]

    table_copies = [
        pltpu.make_async_copy(table_hbm.at[pl.ds(h * NF, NF), :], table_ref.at[pl.ds(h * NF, NF), :], sems.at[h])
        for h in range(2)
    ]
    copies = [
        pltpu.make_async_copy(start_ref.at[:, pl.ds(s * share, share), :], states[s], sems.at[2 + s])
        for s in range(STREAMS)
    ]
    source_copies = [
        pltpu.make_async_copy(
            source_hbm.at[pl.ds(256 * k, 256), :], source_ref.at[pl.ds(256 * k, 256), :], sems.at[2 + STREAMS + k]
        )
        for k in range(4)
    ]
    for c in [table_copies[0], *source_copies, *copies, table_copies[1]]:
        c.start()

    def generate(green, stream, slot):
        own = pl.multiple_of(slot * 16, 16)
        rows = pl.ds(own, 16)
        put = pl.ds(pl.multiple_of(own + stream * share, 16), 16)
        state = states[stream]
        turn, c, s, cp, sp = [state[i, rows, :] for i in range(5)]
        for k in range(BLOCK):
            c, cp = turn * c - cp, c
            s, sp = turn * s - sp, s
            green[k, put, 0:128] = c.astype(BF16)
            green[k, put, 128:256] = s.astype(BF16)
        for i, value in enumerate((c, s, cp, sp)):
            state[i + 1, rows, :] = value

    half_row = lax.broadcasted_iota(jnp.int32, (16, panels), 0) // 8
    for p in range(NCOMP // 2):
        masks[p] = jnp.where(blade_ref[...] == half_row + 2 * p, 1.0, 0.0).astype(BF16)

    def transform(*acc):
        half = NF
        steps = 2 * (tiles // 2) * 4
        per = chunks // STREAMS

        def drain(n, h):
            for m in range(2):
                rows = pltpu.matmul_pop(acc[2 * h + m]).reshape(half // 8, 8, 256)
                spectrum[pl.ds(h * half // 8, half // 8), :, pl.ds((2 * n + m) * 256, 256)] = (
                    jnp.concatenate([rows, rows], axis=1).astype(BF16)
                )

        pending = None
        done = 0
        step = 0
        for n in range(tiles // 2):
            for h in range(2):
                if n == 0:
                    table_copies[h].wait()
                for k in range(4):
                    if n == 0 and h == 0:
                        source_copies[k].wait()
                    for m in range(2):
                        pltpu.matmul_push_rhs(
                            source_ref[pl.ds(256 * k, 256), pl.ds((2 * n + m) * 256, 256)],
                            staging_register=k % 2, mxu_index=m,
                        )
                    for m in range(2):
                        pltpu.matmul_acc_lhs(
                            acc[2 * h + m], table_ref[pl.ds(h * half, half), pl.ds(256 * k, 256)],
                            load_staged_rhs=k % 2,
                        )
                    step += 1
                    if step == 2:
                        for c in copies:
                            c.wait()
                    if step > 2:
                        want = (step - 2) * per // (steps - 2)
                        for slot in range(done, want):
                            for stream in range(STREAMS):
                                generate(green_a, stream, lax.rem(zero + slot, per))
                        done = want
                    if k == 0 and pending is not None:
                        drain(*pending)
                pending = (n, h)
        drain(*pending)

    pl.run_scoped(
        transform,
        pltpu.ACC(0)((NF, 256), F32), pltpu.ACC(1)((NF, 256), F32),
        pltpu.ACC(0)((NF, 256), F32), pltpu.ACC(1)((NF, 256), F32),
    )

    def weigh(q, slot):
        for m in range(2):
            part = spectrum[jnp.minimum(q + m, NF // QUAD - 1)]
            for p in range(NCOMP // 2):
                weighted[2 * slot + m, pl.ds(16 * p, 16), :] = part * masks[p]

    def finish(half_q, m, r):
        total = None
        for b in range(NCOMP):
            top = 8 * b
            u = r[top : top + 8, 0:128]
            v = r[top : top + 8, 128:256]
            w = jnp.where(even, -pltpu.roll(v, 7, 0), pltpu.roll(v, 1, 0))
            z = jnp.where(diagonal, u + w, 0.0)
            if b:
                z = pltpu.roll(z, 2 * b, 0)
            total = z if total is None else total + z
        y = total
        for j in range(1, QUAD):
            y = jnp.where(lane // 32 == j, pltpu.roll(total, 8 - 2 * j, 0), y)
        for b in range(NCOMP):
            out_ref[half_q, b, pl.ds(2 * m, 2), :] = y[2 * b : 2 * b + 2]

    def contract(*acc):
        trips = pairs // GROUP
        local = chunks // trips // STREAMS

        def trip(block, ii, now, later):
            made = 0
            units = [(pair, t) for pair in range(GROUP) for t in range(tiles)]

            def push(pair, t):
                for m in range(2):
                    pltpu.matmul_push_rhs(
                        now[2 * (GROUP * ii + pair) + m, pl.ds(256 * t, 256), :],
                        staging_register=t % 2, mxu_index=m,
                    )

            def accumulate(pair, t):
                for m in range(2):
                    pltpu.matmul_acc_lhs(
                        acc[2 * (pair % 2) + m], weighted[2 * (pair % 2) + m, :, pl.ds(256 * t, 256)],
                        load_staged_rhs=t % 2,
                    )

            def drain(half_q, pair):
                for m in range(2):
                    finish(half_q, m, pltpu.matmul_pop(acc[2 * (pair % 2) + m]))

            def produce(u):
                for n in range(u * local // len(units), (u + 1) * local // len(units)):
                    for stream in range(STREAMS):
                        generate(later, stream, ii * local + lax.rem(zero + n, local))

            for u, (pair, t) in enumerate(units):
                h0 = block * pairs + GROUP * ii + pair
                push(pair, t)
                accumulate(pair, t)
                produce(u)
                if t == POP:
                    weigh(2 * h0 + 2, 1 - pair % 2)
                    if pair:
                        drain(h0 - 1, pair - 1)
            drain(h0, GROUP - 1)

        def step(i, carry):
            def first(ii, c):
                trip(2 * i, ii, green_a, green_b)
                return c

            def second(ii, c):
                trip(2 * i + 1, ii, green_b, green_a)
                return c

            lax.fori_loop(0, trips, first, 0)
            lax.fori_loop(0, trips, second, 0)
            return carry

        for a in acc:
            pltpu.matmul_pop(a)
        weigh(0, 0)
        lax.fori_loop(0, blocks // 2, step, 0)
    pl.run_scoped(contract, *[pltpu.ACC(n % 2)((32, 256), F32) for n in range(4)])


def radiate(table, exchanged, start, blades):
    panels = exchanged.shape[1]
    quads = NF // QUAD
    vm = pl.BlockSpec(memory_space=pltpu.VMEM)
    hbm = pl.BlockSpec(memory_space=pltpu.HBM)
    zero = jnp.minimum(blades[:1], 0)
    return pl.pallas_call(
        radiate_kernel,
        out_shape=jax.ShapeDtypeStruct((quads // 2, NCOMP, 4, 128), F32),
        in_specs=[pl.BlockSpec(memory_space=pltpu.SMEM), hbm, hbm, hbm, vm],
        out_specs=vm,
        scratch_shapes=[
            pltpu.VMEM((2 * NF, NT), BF16),
            pltpu.VMEM((NT, panels), BF16),
            pltpu.VMEM((NF // QUAD, 16, panels), BF16),
            pltpu.VMEM((NCOMP // 2, 16, panels), BF16),
            pltpu.VMEM((4, 32, panels), BF16),
            pltpu.VMEM((BLOCK, panels, 256), BF16),
            pltpu.VMEM((BLOCK, panels, 256), BF16),
            pltpu.SemaphoreType.DMA((6 + STREAMS,)),
        ]
        + [pltpu.VMEM((5, panels // STREAMS, 128), F32)] * STREAMS,
        compiler_params=pltpu.CompilerParams(vmem_limit_bytes=60000000),
        cost_estimate=pl.CostEstimate(flops=20_000_000_000, bytes_accessed=8_000_000, transcendentals=0),
        name="radiate",
    )(zero, table, exchanged, start, blades[None, :])


def regroup_kernel(source_hbm, out_hbm, held, in_sem, out_sem):
    owners, _, width = out_hbm.shape
    parts = 16
    share = owners // parts
    arrive = [
        pltpu.make_async_copy(
            source_hbm.at[:, pl.ds(p * share * width, share * width)],
            held.at[:, pl.ds(p * share * width, share * width)],
            in_sem.at[p],
        )
        for p in range(parts)
    ]
    leave = [
        pltpu.make_async_copy(held.at[:, pl.ds(o * width, width)], out_hbm.at[o], out_sem.at[o])
        for o in range(owners)
    ]
    for c in arrive:
        c.start()
    for p in range(parts):
        arrive[p].wait()
        for o in range(p * share, (p + 1) * share):
            leave[o].start()
    for c in leave:
        c.wait()


def regroup(sources, owners):
    rows, columns = sources.shape
    return pl.pallas_call(
        regroup_kernel,
        out_shape=jax.ShapeDtypeStruct((owners, rows, columns // owners), sources.dtype),
        in_specs=[pl.BlockSpec(memory_space=pltpu.HBM)],
        out_specs=pl.BlockSpec(memory_space=pltpu.HBM),
        scratch_shapes=[
            pltpu.VMEM((rows, columns), sources.dtype),
            pltpu.SemaphoreType.DMA((16,)),
            pltpu.SemaphoreType.DMA((owners,)),
        ],
        compiler_params=pltpu.CompilerParams(vmem_limit_bytes=60_000_000),
        name="regroup",
    )(sources)


def body(sources, panel_pos, panel_blade, observer_table, observer_index):
    owners = lax.axis_size("freq")
    position = lax.axis_index("freq")
    observers = observer_table[:, observer_index]
    width = sources.shape[1] // owners
    blocks = regroup(sources, owners)
    exchanged = lax.all_to_all(blocks, "freq", split_axis=0, concat_axis=0, tiled=True)
    exchanged = exchanged.reshape(-1, width)
    table = transform_table()
    own_pos = lax.dynamic_slice_in_dim(panel_pos, position * width, width, 1)
    own_blade = lax.dynamic_slice_in_dim(panel_blade, position * width, width, 0)
    start = green_start(own_pos, observers)
    partial = radiate(table, exchanged, start, own_blade)
    blocks = partial.reshape(owners * NCOMP, -1, 128).astype(BF16)
    arrived = lax.all_to_all(blocks, ("freq", "grp"), split_axis=0, concat_axis=0, tiled=True)
    total = arrived.astype(F32).sum(0)
    total = total.reshape(-1, 2, QUAD, observers.shape[1]).transpose(0, 2, 1, 3)
    return total.reshape(NF // owners, 1, 2, observers.shape[1])


def solution(mesh):
    in_specs = (P("freq", "grp"), P(None, "grp"), P("grp"), P(), P())
    out_specs = P("freq", "grp", None, None)
    return jax.shard_map(body, mesh=mesh, in_specs=in_specs, out_specs=out_specs, check_vma=False)
```

time: 452 us -> 98.4 us (0.22)
  other arithmetic: 291 us -> 4.95 us
  waiting for transfers between devices: 52.4 us -> 12.1 us
  matrix products: 39.5 us -> 0 us
  Pallas kernels: 0 us -> 36.7 us
  local copies, waits for them, and re-layouts: 29.8 us -> 4.77 us
  blocking collectives: 13.7 us -> 28.3 us
  starting transfers between devices: 18 us -> 10.5 us
  loops' own time: 4.72 us -> 0 us
    another operation x16 -> x0, other arithmetic: 287 us -> none
    all_to_all x2 -> x1, waiting for transfers between devices: 52.4 us -> 12.1 us  [body(): lax.all_to_all(blocks, 'freq', split_axis=0, concat_axis=0, tiled=True)]
    dot_general x9 -> x0, matrix products: 39.5 us -> none  [the longest x1 21.4 us: body(): jnp.dot(dft_table, exchanged, preferred_element_type=jnp.float32)]
    pallas_call x0 -> x3, Pallas kernels: none -> 36.7 us  [the longest x1 26.4 us: radiate(): pl.pallas_call(radiate_kernel, out_shape=jax.ShapeDtypeStruct((quads // 2...]
    all_to_all x0 -> x1, blocking collectives: none -> 28.3 us  [body(): lax.all_to_all(blocks, ('freq', 'grp'), split_axis=0, concat_axis=0, tile...]
    all_gather x1 -> x0, blocking collectives: 13.7 us -> none  [over_pieces(): return lax.all_gather(x, axis).sum(0)]
    slice x10 -> x1, local copies, waits for them, and re-layouts: 13 us -> 0.5 us  [radiate(): zero = jnp.minimum(blades[:1], 0)]
    all_to_all x2 -> x1, starting transfers between devices: 18 us -> 10.5 us  [body(): lax.all_to_all(blocks, 'freq', split_axis=0, concat_axis=0, tiled=True)]
  transfers between devices with their start and end apart: 2 -> 1, of which waited for: 2 -> 1; matrix products, arithmetic and copies ran while one was open for 1% -> 6% of each run, Pallas kernels for 0% -> 7%
where the time goes in v2:
time: 98.4 us; the launch traced here: 98 us
  Pallas kernels  36.7 us (37%)
  blocking collectives  28.3 us (29%)
  waiting for transfers between devices  12.1 us (12%)
  starting transfers between devices  10.5 us (11%)
  other arithmetic  4.95 us (5%)
  local copies, waits for them, and re-layouts  4.77 us (5%)
    all_to_all x1, blocking collectives, body(): lax.all_to_all(blocks, ('freq', 'grp'), split_axis=0, concat_axis=0, tile...  28.3 us
    pallas_call x1, Pallas kernels, radiate(): pl.pallas_call(radiate_kernel, out_shape=jax.ShapeDtypeStruct((quads // 2...  26.4 us
    all_to_all x1, waiting for transfers between devices, body(): lax.all_to_all(blocks, 'freq', split_axis=0, concat_axis=0, tiled=True)  12.1 us
    all_to_all x1, starting transfers between devices, body(): lax.all_to_all(blocks, 'freq', split_axis=0, concat_axis=0, tiled=True)  10.5 us
    pallas_call x1, Pallas kernels, green_start(): pl.pallas_call(prepare_kernel, out_shape=jax.ShapeDtypeStruct((5, panels,...  7.11 us
    pallas_call x1, Pallas kernels, regroup(): pl.pallas_call(regroup_kernel, out_shape=jax.ShapeDtypeStruct((owners, ro...  3.17 us
    unnamed x12, local copies, waits for them, and re-layouts  2.11 us
    convert_element_type x1, other arithmetic, transform_table(): return rows.astype(BF16).reshape(2 * NF, NT)  2.06 us
  transfers between devices with their start and end apart: 1, of which 1 were waited for; matrix products, arithmetic and copies ran while one was open for 6% of the time, Pallas kernels for 7%

profile of v2, /device:TPU:1, one launch (start us, length us, event | category | flops | bytes accessed | tf_op | source)
XLA Modules:
  0.0 98.0 jit_solution(15410401709096080498)
XLA Ops:
  0.0 0.0 copy-start
  0.0 3.2 %regroup.1 = bf16[64,16,1024]{2,1,0:T(8,128)(2,1)} custom-call(bf16[16,65536]{1,0:T(8,128)(2,1)} %source_hbm.1), custom_call_target="tpu_custom_call" | custom-call | tf_op jit(solution)/shard_map/regroup/pallas_call | solution.py:335
  3.2 0.0 copy-start.2
  3.2 0.0 copy-start.4
  3.2 10.5 %all-to-all-start = ((bf16[64,16,1024]{2,1,0:T(8,128)(2,1)}), bf16[64,16,1024]{2,1,0:T(8,128)(2,1)}, u32[]{:S(2)}, u32[]{:S(2)}) async-start(bf16[64,16,1024]{2,1,0:T(8,128)(2,1)} %regroup.1), calls=%async_computation | async-start | bytes 4194304 | tf_op jit(solution)/shard_map/all_to_all | solution.py:356
  13.8 0.7 dynamic_slice.6
  14.4 0.0 copy-start.3
  14.4 0.5 slice.3
  15.0 0.3 sine_multiply_fusion
  15.3 1.1 %fusion.3 = (f32[64,1024]{1,0:T(8,128)S(1)}, f32[64,1024]{1,0:T(8,128)S(1)}) fusion(s32[64]{0:T(128)S(1)} %get-tuple-element.18, s32[64]{0:T(128)S(1)} %get-tuple-element.17), kind=kLoop, calls=%fused_computation.9 | loop fusion | flops 983040 | bytes 524800 | tf_op jit(solution)/shard_map/sin | solution.py:34
  16.4 0.0 copy-done
  16.5 0.2 copy.17
  16.7 0.0 copy-done.2
  16.7 0.4 copy.13
  17.1 0.0 copy-done.4
  17.1 0.6 gather_fusion
  17.7 0.1 copy.14
  17.8 0.1 tile.10.observer_ref
  18.4 7.1 %prepare.1.start_ref = f32[5,1024,128]{2,1,0:T(8,128)S(1)} custom-call(f32[1024,3]{1,0:T(8,128)S(1)} %bitcast.8, f32[3,128]{1,0:T(4,128)S(1)} %tile.10.observer_ref), custom_call_target="tpu_custom_call" | custom-call | flops 20000000 | bytes 3000000 | tf_op jit(solution)/shard_map/prepare/pallas_call | solution.py:79
  25.5 0.0 copy-done.3
  25.6 0.0 copy-start.1
  25.6 1.5 %copy-done.1 = f32[5,1024,128]{2,1,0:T(8,128)} copy-done((f32[5,1024,128]{2,1,0:T(8,128)}, f32[5,1024,128]{2,1,0:T(8,128)S(1)}, u32[]{:S(2)}) %copy-start.1) | copy-done | bytes 2621464
  27.1 2.1 %subtract_convert_fusion = bf16[16,64,1024]{2,1,0:T(8,128)(2,1)} fusion(f32[64,1024]{1,0:T(8,128)S(1)} %get-tuple-element.12, f32[16,1024]{1,0:T(8,128)S(1)} %get-tuple-element.11, f32[64,1024]{1,0:T(8,128)S(1)} %get-tuple-element.10, f32[16,1024]{1,0:T(8,128)S(1)} %get-tuple-element.9), kind=kLoop, calls=%fused_computation.1 | loop fusion | flops 4194304 | bytes 2752512 | tf_op jit(solution)/shard_map/convert_element_type | solution.py:38
  29.1 12.1 %all-to-all-done = bf16[64,16,1024]{2,1,0:T(8,128)(2,1)} async-done(((bf16[64,16,1024]{2,1,0:T(8,128)(2,1)}), bf16[64,16,1024]{2,1,0:T(8,128)(2,1)}, u32[]{:S(2)}, u32[]{:S(2)}) %all-to-all-start) | async-done | bytes 2097184 | tf_op jit(solution)/shard_map/all_to_all | solution.py:356
  41.2 26.4 %radiate.1 = f32[64,4,4,128]{3,2,1,0:T(4,128)} custom-call(s32[1]{0:T(128)S(6)} %min.3.zero_ref, bf16[1024,1024]{1,0:T(8,128)(2,1)} %bitcast.9, bf16[1024,1024]{1,0:T(8,128)(2,1)} %bitcast.1.source_hbm, f32[5,1024,128]{2,1,0:T(8,128)} %copy-done.1, s32[1,1024]{1,0:T(1,128)} %bitcast.14), custom_call_target="tpu_custom_call" | custom-call | flops 20000000000 | bytes 8000000 | tf_op jit(solution)/shard_map/radiate/pallas_call | solution.py:285
  67.6 1.1 %convert_element_type.30 = bf16[64,4,4,128]{3,2,1,0:T(4,128)(2,1)S(1)} convert(f32[64,4,4,128]{3,2,1,0:T(4,128)} %radiate.1) | non-fusion elementwise | flops 131072 | bytes 786432 | tf_op jit(solution)/shard_map/convert_element_type | solution.py:363
  68.7 28.3 %all_to_all.10 = bf16[256,4,128]{2,1,0:T(4,128)(2,1)S(1)} all-to-all(bf16[256,4,128]{2,1,0:T(4,128)(2,1)S(1)} %bitcast.10), channel_id=1, replica_groups=mesh['grp'=4,'freq'=64] {'freq','grp'}, dimensions={0} | all-to-all | bytes 524288 | tf_op jit(solution)/shard_map/all_to_all | solution.py:364
  97.0 0.3 convert_reduce_fusion
  97.3 0.1 reshape.58
  97.4 0.6 copy.16
  (7 shorter events, 0.0 us)
Async XLA Ops:
  0.0 16.4 %copy-start = (f32[3,65536]{1,0:T(4,128)S(1)}, f32[3,65536]{1,0:T(4,128)}, u32[]{:S(2)}) copy-start(f32[3,65536]{1,0:T(4,128)} %param.6) | copy-start | bytes 2359300
  3.2 13.5 %copy-start.2 = (f32[3,2048]{1,0:T(4,128)S(1)}, f32[3,2048]{1,0:T(4,128)}, u32[]{:S(2)}) copy-start(f32[3,2048]{1,0:T(4,128)} %param.8) | copy-start | bytes 73732
  3.2 13.9 %copy-start.4 = (s32[32]{0:T(128)S(1)}, s32[32]{0:T(128)}, u32[]{:S(2)}) copy-start(s32[32]{0:T(128)} %param.9) | copy-start | bytes 388
  3.2 38.0 %all-to-all-start = ((bf16[64,16,1024]{2,1,0:T(8,128)(2,1)}), bf16[64,16,1024]{2,1,0:T(8,128)(2,1)}, u32[]{:S(2)}, u32[]{:S(2)}) async-start(bf16[64,16,1024]{2,1,0:T(8,128)(2,1)} %regroup.1), calls=%async_computation | async-start | bytes 4194304 | tf_op jit(solution)/shard_map/all_to_all | solution.py:356
  14.4 11.1 %copy-start.3 = (s32[1024]{0:T(1024)}, s32[1024]{0:T(1024)S(1)}, u32[]{:S(2)}) copy-start(s32[1024]{0:T(1024)S(1)} %dynamic_slice.6) | copy-start | bytes 12292
  25.6 1.5 %copy-start.1 = (f32[5,1024,128]{2,1,0:T(8,128)}, f32[5,1024,128]{2,1,0:T(8,128)S(1)}, u32[]{:S(2)}) copy-start(f32[5,1024,128]{2,1,0:T(8,128)S(1)} %prepare.1.start_ref) | copy-start | bytes 7864324

commit v3 on v2

--- a/solution.py
+++ b/solution.py
@@ -15,6 +15,7 @@
 BLOCK = 16
 STREAMS = 2
 GROUP = 2
+EARLY = 64
 POP = 1
 F32, BF16 = jnp.float32, jnp.bfloat16
 
@@ -38,58 +39,70 @@
     return rows.astype(BF16).reshape(2 * NF, NT)
 
 
-def prepare_kernel(column_ref, observer_ref, out_ref):
-    offset = (lax.broadcasted_iota(jnp.int32, (16, 128), 1) // 32 - QUAD).astype(F32) * wave_step
-    observers = [jnp.broadcast_to(observer_ref[i : i + 1, :], (16, 128)) for i in range(3)]
+def prepare_kernel(column_ref, observer_ref, state_ref, green_ref):
+    size = column_ref.shape[0]
+    offset = (lax.broadcasted_iota(jnp.int32, (size, 128), 1) // 32 - QUAD).astype(F32) * wave_step
 
     def cos_sin(x):
         x2 = x * x
-        c, s = 1.0 / math.factorial(14), 1.0 / math.factorial(15)
-        c, s = -c, -s
+        c, s = -1.0 / math.factorial(14), -1.0 / math.factorial(15)
         for n in range(6, -1, -1):
             sign = 1.0 if n % 2 == 0 else -1.0
             c = c * x2 + sign / math.factorial(2 * n)
             s = s * x2 + sign / math.factorial(2 * n + 1)
         return c, s * x
 
+    square = None
+    for axis in range(3):
+        diff = observer_ref[axis : axis + 1, :] - column_ref[:, axis : axis + 1]
+        square = diff * diff if square is None else square + diff * diff
+    distance = jnp.sqrt(square)
+    amplitude = 0.25 / (math.pi * distance)
+    cn, sn = cos_sin(offset * distance)
+    cq, sq = cos_sin((wave_step * QUAD) * distance)
+    c, s = cn * amplitude, -sn * amplitude
+    for n, value in enumerate((2.0 * cq, c, s, c * cq - s * sq, s * cq + c * sq)):
+        state_ref[n] = value
+
     def step(i, carry):
-        rows = pl.ds(pl.multiple_of(16 * i, 16), 16)
-        square = None
-        for axis in range(3):
-            diff = observers[axis] - column_ref[rows, axis : axis + 1]
-            square = diff * diff if square is None else square + diff * diff
-        distance = jnp.sqrt(square)
-        amplitude = 0.25 / (math.pi * distance)
-        cn, sn = cos_sin(offset * distance)
-        cq, sq = cos_sin((wave_step * QUAD) * distance)
-        c1, s1 = cn * amplitude, -sn * amplitude
-        out_ref[0, rows, :] = 2.0 * cq
-        out_ref[1, rows, :] = c1
-        out_ref[2, rows, :] = s1
-        out_ref[3, rows, :] = c1 * cq - s1 * sq
-        out_ref[4, rows, :] = s1 * cq + c1 * sq
+        rows = pl.ds(pl.multiple_of(32 * i, 32), 32)
+        turn, c, s, cp, sp = [state_ref[n, rows, :] for n in range(5)]
+        for k in range(EARLY):
+            c, cp = turn * c - cp, c
+            s, sp = turn * s - sp, s
+            green_ref[k, rows, 0:128] = c.astype(BF16)
+            green_ref[k, rows, 128:256] = s.astype(BF16)
+        for n, value in enumerate((c, s, cp, sp)):
+            state_ref[n + 1, rows, :] = value
         return carry
 
-    lax.fori_loop(0, out_ref.shape[1] // 16, step, 0)
+    lax.fori_loop(0, size // 32, step, 0)
 
 
 def green_start(positions, observers):
     panels = positions.shape[1]
-    vm = pl.BlockSpec(memory_space=pltpu.VMEM)
+    size = 128
     return pl.pallas_call(
         prepare_kernel,
-        out_shape=jax.ShapeDtypeStruct((5, panels, 128), F32),
-        in_specs=[vm, vm],
-        out_specs=vm,
-        compiler_params=pltpu.CompilerParams(vmem_limit_bytes=8 * 1024 * 1024),
-        cost_estimate=pl.CostEstimate(flops=20_000_000, bytes_accessed=3_000_000, transcendentals=0),
+        grid=(panels // size,),
+        out_shape=(
+            jax.ShapeDtypeStruct((5, panels, 128), F32),
+            jax.ShapeDtypeStruct((EARLY, panels, 256), BF16),
+        ),
+        in_specs=[pl.BlockSpec((size, 3), lambda i: (i, 0)), pl.BlockSpec((3, 128), lambda i: (0, 0))],
+        out_specs=(
+            pl.BlockSpec((5, size, 128), lambda i: (0, i, 0)),
+            pl.BlockSpec((EARLY, size, 256), lambda i: (0, i, 0)),
+        ),
+        compiler_params=pltpu.CompilerParams(vmem_limit_bytes=42_000_000),
+        cost_estimate=pl.CostEstimate(flops=5_000_000_000, bytes_accessed=36_000_000, transcendentals=0),
         name="prepare",
     )(positions.T, jnp.tile(observers, (1, QUAD)))
 
 
 def radiate_kernel(
-    zero_ref, table_hbm, source_hbm, start_ref, blade_ref, out_ref,
-    table_ref, source_ref, spectrum, masks, weighted, green_a, green_b, sems, *states
+    zero_ref, table_hbm, source_hbm, start_ref, early_hbm, blade_ref, out_ref,
+    table_ref, source_ref, spectrum, masks, weighted, held, green_b, sems, *states
 ):
     panels = source_ref.shape[1]
     share = panels // STREAMS
@@ -111,13 +124,17 @@
         pltpu.make_async_copy(start_ref.at[:, pl.ds(s * share, share), :], states[s], sems.at[2 + s])
         for s in range(STREAMS)
     ]
+    def early_copy(i):
+        slot = lax.rem(i, 2)
+        return pltpu.make_async_copy(early_hbm.at[pl.ds(i * BLOCK, BLOCK)], held.at[slot], sems.at[6 + STREAMS + slot])
+
     source_copies = [
         pltpu.make_async_copy(
             source_hbm.at[pl.ds(256 * k, 256), :], source_ref.at[pl.ds(256 * k, 256), :], sems.at[2 + STREAMS + k]
         )
         for k in range(4)
     ]
-    for c in [table_copies[0], *source_copies, *copies, table_copies[1]]:
+    for c in [table_copies[0], *source_copies, table_copies[1], early_copy(zero), *copies]:
         c.start()
 
     def generate(green, stream, slot):
@@ -140,8 +157,6 @@
 
     def transform(*acc):
         half = NF
-        steps = 2 * (tiles // 2) * 4
-        per = chunks // STREAMS
 
         def drain(n, h):
             for m in range(2):
@@ -151,8 +166,6 @@
                 )
 
         pending = None
-        done = 0
-        step = 0
         for n in range(tiles // 2):
             for h in range(2):
                 if n == 0:
@@ -170,16 +183,6 @@
                             acc[2 * h + m], table_ref[pl.ds(h * half, half), pl.ds(256 * k, 256)],
                             load_staged_rhs=k % 2,
                         )
-                    step += 1
-                    if step == 2:
-                        for c in copies:
-                            c.wait()
-                    if step > 2:
-                        want = (step - 2) * per // (steps - 2)
-                        for slot in range(done, want):
-                            for stream in range(STREAMS):
-                                generate(green_a, stream, lax.rem(zero + slot, per))
-                        done = want
                     if k == 0 and pending is not None:
                         drain(*pending)
                 pending = (n, h)
@@ -197,7 +200,10 @@
             for p in range(NCOMP // 2):
                 weighted[2 * slot + m, pl.ds(16 * p, 16), :] = part * masks[p]
 
-    def finish(half_q, m, r):
+    def merge(a, b, c, d):
+        return jnp.where(row < 4, jnp.where(row < 2, a, b), jnp.where(row < 6, c, d))
+
+    def finish(r):
         total = None
         for b in range(NCOMP):
             top = 8 * b
@@ -211,14 +217,13 @@
         y = total
         for j in range(1, QUAD):
             y = jnp.where(lane // 32 == j, pltpu.roll(total, 8 - 2 * j, 0), y)
-        for b in range(NCOMP):
-            out_ref[half_q, b, pl.ds(2 * m, 2), :] = y[2 * b : 2 * b + 2]
+        return y
 
     def contract(*acc):
         trips = pairs // GROUP
         local = chunks // trips // STREAMS
 
-        def trip(block, ii, now, later):
+        def trip(block, ii, now, later=None):
             made = 0
             units = [(pair, t) for pair in range(GROUP) for t in range(tiles)]
 
@@ -237,10 +242,14 @@
                     )
 
             def drain(half_q, pair):
-                for m in range(2):
-                    finish(half_q, m, pltpu.matmul_pop(acc[2 * (pair % 2) + m]))
+                y0, y1 = [finish(pltpu.matmul_pop(acc[2 * (pair % 2) + m])) for m in range(2)]
+                upper = merge(y0, pltpu.roll(y1, 2, 0), pltpu.roll(y0, 2, 0), pltpu.roll(y1, 4, 0))
+                lower = merge(pltpu.roll(y0, 4, 0), pltpu.roll(y1, 6, 0), pltpu.roll(y0, 6, 0), y1)
+                out_ref[half_q] = jnp.concatenate([upper, lower], axis=0).astype(BF16)
 
             def produce(u):
+                if later is None:
+                    return
                 for n in range(u * local // len(units), (u + 1) * local // len(units)):
                     for stream in range(STREAMS):
                         generate(later, stream, ii * local + lax.rem(zero + n, local))
@@ -257,18 +266,29 @@
             drain(h0, GROUP - 1)
 
         def step(i, carry):
+            @pl.when(i + 1 < blocks // 2)
+            def _():
+                early_copy(i + 1).start()
+
+            early_copy(i).wait()
+
             def first(ii, c):
-                trip(2 * i, ii, green_a, green_b)
+                trip(i, ii, held.at[lax.rem(i, 2)], green_b)
                 return c
 
+            lax.fori_loop(0, trips, first, 0)
+            weigh((blocks // 2 + i) * BLOCK, 0)
+
             def second(ii, c):
-                trip(2 * i + 1, ii, green_b, green_a)
+                trip(blocks // 2 + i, ii, green_b)
                 return c
 
-            lax.fori_loop(0, trips, first, 0)
             lax.fori_loop(0, trips, second, 0)
+            weigh((i + 1) * BLOCK, 0)
             return carry
 
+        for c in copies:
+            c.wait()
         for a in acc:
             pltpu.matmul_pop(a)
         weigh(0, 0)
@@ -277,6 +297,7 @@
 
 
 def radiate(table, exchanged, start, blades):
+    start, early = start
     panels = exchanged.shape[1]
     quads = NF // QUAD
     vm = pl.BlockSpec(memory_space=pltpu.VMEM)
@@ -284,8 +305,8 @@
     zero = jnp.minimum(blades[:1], 0)
     return pl.pallas_call(
         radiate_kernel,
-        out_shape=jax.ShapeDtypeStruct((quads // 2, NCOMP, 4, 128), F32),
-        in_specs=[pl.BlockSpec(memory_space=pltpu.SMEM), hbm, hbm, hbm, vm],
+        out_shape=jax.ShapeDtypeStruct((quads // 2, 4 * NCOMP, 128), BF16),
+        in_specs=[pl.BlockSpec(memory_space=pltpu.SMEM), hbm, hbm, hbm, hbm, vm],
         out_specs=vm,
         scratch_shapes=[
             pltpu.VMEM((2 * NF, NT), BF16),
@@ -293,15 +314,15 @@
             pltpu.VMEM((NF // QUAD, 16, panels), BF16),
             pltpu.VMEM((NCOMP // 2, 16, panels), BF16),
             pltpu.VMEM((4, 32, panels), BF16),
+            pltpu.VMEM((2, BLOCK, panels, 256), BF16),
             pltpu.VMEM((BLOCK, panels, 256), BF16),
-            pltpu.VMEM((BLOCK, panels, 256), BF16),
-            pltpu.SemaphoreType.DMA((6 + STREAMS,)),
+            pltpu.SemaphoreType.DMA((8 + STREAMS,)),
         ]
         + [pltpu.VMEM((5, panels // STREAMS, 128), F32)] * STREAMS,
         compiler_params=pltpu.CompilerParams(vmem_limit_bytes=60000000),
         cost_estimate=pl.CostEstimate(flops=20_000_000_000, bytes_accessed=8_000_000, transcendentals=0),
         name="radiate",
-    )(zero, table, exchanged, start, blades[None, :])
+    )(zero, table, exchanged, start, early, blades[None, :])
 
 
 def regroup_kernel(source_hbm, out_hbm, held, in_sem, out_sem):
@@ -360,7 +381,7 @@
     own_blade = lax.dynamic_slice_in_dim(panel_blade, position * width, width, 0)
     start = green_start(own_pos, observers)
     partial = radiate(table, exchanged, start, own_blade)
-    blocks = partial.reshape(owners * NCOMP, -1, 128).astype(BF16)
+    blocks = partial.reshape(owners * NCOMP, -1, 128)
     arrived = lax.all_to_all(blocks, ("freq", "grp"), split_axis=0, concat_axis=0, tiled=True)
     total = arrived.astype(F32).sum(0)
     total = total.reshape(-1, 2, QUAD, observers.shape[1]).transpose(0, 2, 1, 3)

time: 98.4 us -> 94.9 us (0.964)
  waiting for transfers between devices: 12.1 us -> 5.14 us
  Pallas kernels: 36.7 us -> 40.9 us
  other arithmetic: 4.95 us -> 3.79 us
    all_to_all x1, waiting for transfers between devices: 12.1 us -> 5.14 us  [body(): lax.all_to_all(blocks, 'freq', split_axis=0, concat_axis=0, tiled=True)]
    pallas_call x1, Pallas kernels: 7.11 us -> 13.9 us  [green_start(): pl.pallas_call(prepare_kernel, grid=(panels // size,), out_shape=(jax.Sha...]
    pallas_call x1, Pallas kernels: 26.4 us -> 23.8 us  [radiate(): pl.pallas_call(radiate_kernel, out_shape=jax.ShapeDtypeStruct((quads // 2...]
    convert_element_type x1 -> x0, other arithmetic: 1.13 us -> none  [body(): blocks = partial.reshape(owners * NCOMP, -1, 128).astype(BF16)]
  transfers between devices with their start and end apart: 1 -> 1, of which waited for: 1 -> 1; matrix products, arithmetic and copies ran while one was open for 6% -> 6% of each run, Pallas kernels for 7% -> 15%
where the time goes in v3:
time: 94.9 us; the launch traced here: 94.6 us
  Pallas kernels  40.9 us (43%)
  blocking collectives  28.7 us (30%)
  starting transfers between devices  10.5 us (11%)
  waiting for transfers between devices  5.14 us (5%)
  local copies, waits for them, and re-layouts  4.79 us (5%)
  other arithmetic  3.79 us (4%)
    all_to_all x1, blocking collectives, body(): lax.all_to_all(blocks, ('freq', 'grp'), split_axis=0, concat_axis=0, tile...  28.7 us
    pallas_call x1, Pallas kernels, radiate(): pl.pallas_call(radiate_kernel, out_shape=jax.ShapeDtypeStruct((quads // 2...  23.8 us
    pallas_call x1, Pallas kernels, green_start(): pl.pallas_call(prepare_kernel, grid=(panels // size,), out_shape=(jax.Sha...  13.9 us
    all_to_all x1, starting transfers between devices, body(): lax.all_to_all(blocks, 'freq', split_axis=0, concat_axis=0, tiled=True)  10.5 us
    all_to_all x1, waiting for transfers between devices, body(): lax.all_to_all(blocks, 'freq', split_axis=0, concat_axis=0, tiled=True)  5.14 us
    pallas_call x1, Pallas kernels, regroup(): pl.pallas_call(regroup_kernel, out_shape=jax.ShapeDtypeStruct((owners, ro...  3.1 us
    unnamed x12, local copies, waits for them, and re-layouts  2.07 us
    convert_element_type x1, other arithmetic, transform_table(): return rows.astype(BF16).reshape(2 * NF, NT)  2.03 us
  transfers between devices with their start and end apart: 1, of which 1 were waited for; matrix products, arithmetic and copies ran while one was open for 6% of the time, Pallas kernels for 15%

profile of v3, /device:TPU:1, one launch (start us, length us, event | category | flops | bytes accessed | tf_op | source)
XLA Modules:
  0.0 94.6 jit_solution(6450323374660138317)
XLA Ops:
  0.0 0.0 copy-start
  0.0 0.0 copy-start.2
  0.0 3.1 %regroup.1 = bf16[64,16,1024]{2,1,0:T(8,128)(2,1)} custom-call(bf16[16,65536]{1,0:T(8,128)(2,1)} %source_hbm.1), custom_call_target="tpu_custom_call" | custom-call | tf_op jit(solution)/shard_map/regroup/pallas_call | solution.py:356
  3.1 0.0 copy-start.4
  3.1 10.5 %all-to-all-start = ((bf16[64,16,1024]{2,1,0:T(8,128)(2,1)}), bf16[64,16,1024]{2,1,0:T(8,128)(2,1)}, u32[]{:S(2)}, u32[]{:S(2)}) async-start(bf16[64,16,1024]{2,1,0:T(8,128)(2,1)} %regroup.1), calls=%async_computation | async-start | bytes 4194304 | tf_op jit(solution)/shard_map/all_to_all | solution.py:377
  13.7 0.7 dynamic_slice.6
  14.4 0.0 copy-start.3
  14.4 0.6 slice.3
  14.9 0.0 copy-done
  15.0 0.2 copy.17
  15.2 0.3 sine_multiply_fusion
  15.6 1.1 %fusion.3 = (f32[64,1024]{1,0:T(8,128)S(1)}, f32[64,1024]{1,0:T(8,128)S(1)}) fusion(s32[64]{0:T(128)S(1)} %get-tuple-element.22, s32[64]{0:T(128)S(1)} %get-tuple-element.21), kind=kLoop, calls=%fused_computation.9 | loop fusion | flops 983040 | bytes 524800 | tf_op jit(solution)/shard_map/sin | solution.py:35
  16.7 0.0 copy-done.2
  16.7 0.4 copy.13
  17.1 0.0 copy-done.4
  17.1 0.6 gather_fusion
  17.7 0.1 copy.14
  17.7 0.1 tile.10.observer_ref
  18.5 2.0 %subtract_convert_fusion = bf16[16,64,1024]{2,1,0:T(8,128)(2,1)} fusion(f32[64,1024]{1,0:T(8,128)S(1)} %get-tuple-element.14, f32[16,1024]{1,0:T(8,128)S(1)} %get-tuple-element.13, f32[64,1024]{1,0:T(8,128)S(1)} %get-tuple-element.12, f32[16,1024]{1,0:T(8,128)S(1)} %get-tuple-element.11), kind=kLoop, calls=%fused_computation.1 | loop fusion | flops 4194304 | bytes 2752512 | tf_op jit(solution)/shard_map/convert_element_type | solution.py:39
  20.6 13.9 %prepare.1 = (f32[5,1024,128]{2,1,0:T(8,128)S(1)}, bf16[64,1024,256]{2,1,0:T(8,128)(2,1)}) custom-call(f32[1024,3]{1,0:T(8,128)S(1)} %bitcast.8, f32[3,128]{1,0:T(4,128)S(1)} %tile.10.observer_ref), custom_call_target="tpu_custom_call" | custom-call | flops 5000000000 | bytes 36000000 | tf_op jit(solution)/shard_map/prepare/pallas_call | solution.py:85
  34.5 0.0 copy-done.3
  34.5 0.0 copy-start.1
  34.5 1.5 %copy-done.1 = f32[5,1024,128]{2,1,0:T(8,128)} copy-done((f32[5,1024,128]{2,1,0:T(8,128)}, f32[5,1024,128]{2,1,0:T(8,128)S(1)}, u32[]{:S(2)}) %copy-start.1) | copy-done | bytes 2621464
  36.0 5.1 %all-to-all-done = bf16[64,16,1024]{2,1,0:T(8,128)(2,1)} async-done(((bf16[64,16,1024]{2,1,0:T(8,128)(2,1)}), bf16[64,16,1024]{2,1,0:T(8,128)(2,1)}, u32[]{:S(2)}, u32[]{:S(2)}) %all-to-all-start) | async-done | bytes 2097184 | tf_op jit(solution)/shard_map/all_to_all | solution.py:377
  41.1 23.8 %radiate.1 = bf16[64,16,128]{2,1,0:T(8,128)(2,1)} custom-call(s32[1]{0:T(128)S(6)} %min.3.zero_ref, bf16[1024,1024]{1,0:T(8,128)(2,1)} %bitcast.9, bf16[1024,1024]{1,0:T(8,128)(2,1)} %bitcast.1.source_hbm, f32[5,1024,128]{2,1,0:T(8,128)} %copy-done.1, bf16[64,1024,256]{2,1,0:T(8,128)(2,1)} %get-tuple-element.16.early_hbm, s32[1,1024]{1,0:T(1,128)} %bitcast.14), custom_call_target="tpu_custom_call" | custom-call | flops 20000000000 | bytes 8000000 | tf_op jit(solution)/shard_map/radiate/pallas_call | solution.py:306
  65.0 28.7 %all_to_all.10 = bf16[256,4,128]{2,1,0:T(4,128)(2,1)S(1)} all-to-all(bf16[256,4,128]{2,1,0:T(4,128)(2,1)} %bitcast.10), channel_id=1, replica_groups=mesh['grp'=4,'freq'=64] {'freq','grp'}, dimensions={0} | all-to-all | bytes 524288 | tf_op jit(solution)/shard_map/all_to_all | solution.py:385
  93.6 0.3 convert_reduce_fusion
  93.9 0.1 reshape.60
  94.0 0.6 copy.16
  (7 shorter events, 0.0 us)
Async XLA Ops:
  0.0 14.9 %copy-start = (f32[3,65536]{1,0:T(4,128)S(1)}, f32[3,65536]{1,0:T(4,128)}, u32[]{:S(2)}) copy-start(f32[3,65536]{1,0:T(4,128)} %param.6) | copy-start | bytes 2359300
  0.0 16.7 %copy-start.2 = (f32[3,2048]{1,0:T(4,128)S(1)}, f32[3,2048]{1,0:T(4,128)}, u32[]{:S(2)}) copy-start(f32[3,2048]{1,0:T(4,128)} %param.8) | copy-start | bytes 73732
  3.1 13.9 %copy-start.4 = (s32[32]{0:T(128)S(1)}, s32[32]{0:T(128)}, u32[]{:S(2)}) copy-start(s32[32]{0:T(128)} %param.9) | copy-start | bytes 388
  3.1 38.0 %all-to-all-start = ((bf16[64,16,1024]{2,1,0:T(8,128)(2,1)}), bf16[64,16,1024]{2,1,0:T(8,128)(2,1)}, u32[]{:S(2)}, u32[]{:S(2)}) async-start(bf16[64,16,1024]{2,1,0:T(8,128)(2,1)} %regroup.1), calls=%async_computation | async-start | bytes 4194304 | tf_op jit(solution)/shard_map/all_to_all | solution.py:377
  14.4 20.1 %copy-start.3 = (s32[1024]{0:T(1024)}, s32[1024]{0:T(1024)S(1)}, u32[]{:S(2)}) copy-start(s32[1024]{0:T(1024)S(1)} %dynamic_slice.6) | copy-start | bytes 12292
  34.5 1.5 %copy-start.1 = (f32[5,1024,128]{2,1,0:T(8,128)}, f32[5,1024,128]{2,1,0:T(8,128)S(1)}, u32[]{:S(2)}) copy-start(f32[5,1024,128]{2,1,0:T(8,128)S(1)} %get-tuple-element.15.start_ref) | copy-start | bytes 7864324

commit v4 on v3

--- a/solution.py
+++ b/solution.py
@@ -14,7 +14,7 @@
 QUAD = 4
 BLOCK = 16
 STREAMS = 2
-GROUP = 2
+GROUP = 4
 EARLY = 64
 POP = 1
 F32, BF16 = jnp.float32, jnp.bfloat16
@@ -223,14 +223,14 @@
         trips = pairs // GROUP
         local = chunks // trips // STREAMS
 
-        def trip(block, ii, now, later=None):
+        def trip(block, ii, group, now, later=None):
             made = 0
-            units = [(pair, t) for pair in range(GROUP) for t in range(tiles)]
+            units = [(pair, t) for pair in range(group) for t in range(tiles)]
 
             def push(pair, t):
                 for m in range(2):
                     pltpu.matmul_push_rhs(
-                        now[2 * (GROUP * ii + pair) + m, pl.ds(256 * t, 256), :],
+                        now[2 * (group * ii + pair) + m, pl.ds(256 * t, 256), :],
                         staging_register=t % 2, mxu_index=m,
                     )
 
@@ -255,7 +255,7 @@
                         generate(later, stream, ii * local + lax.rem(zero + n, local))
 
             for u, (pair, t) in enumerate(units):
-                h0 = block * pairs + GROUP * ii + pair
+                h0 = block * pairs + group * ii + pair
                 push(pair, t)
                 accumulate(pair, t)
                 produce(u)
@@ -263,7 +263,7 @@
                     weigh(2 * h0 + 2, 1 - pair % 2)
                     if pair:
                         drain(h0 - 1, pair - 1)
-            drain(h0, GROUP - 1)
+            drain(h0, group - 1)
 
         def step(i, carry):
             @pl.when(i + 1 < blocks // 2)
@@ -273,17 +273,13 @@
             early_copy(i).wait()
 
             def first(ii, c):
-                trip(i, ii, held.at[lax.rem(i, 2)], green_b)
+                trip(i, ii, GROUP, held.at[lax.rem(i, 2)], green_b)
                 return c
 
             lax.fori_loop(0, trips, first, 0)
             weigh((blocks // 2 + i) * BLOCK, 0)
 
-            def second(ii, c):
-                trip(blocks // 2 + i, ii, green_b)
-                return c
-
-            lax.fori_loop(0, trips, second, 0)
+            trip(blocks // 2 + i, 0, pairs, green_b)
             weigh((i + 1) * BLOCK, 0)
             return carry
 

time: 94.9 us -> 93.3 us (0.983)
  Pallas kernels: 40.9 us -> 39.2 us
    pallas_call x1, Pallas kernels: 23.8 us -> 22.2 us  [radiate(): pl.pallas_call(radiate_kernel, out_shape=jax.ShapeDtypeStruct((quads // 2...]
  transfers between devices with their start and end apart: 1 -> 1, of which waited for: 1 -> 1; matrix products, arithmetic and copies ran while one was open for 6% -> 7% of each run, Pallas kernels for 15% -> 15%
where the time goes in v4:
time: 93.3 us; the launch traced here: 93 us
  Pallas kernels  39.2 us (42%)
  blocking collectives  28.7 us (31%)
  starting transfers between devices  10.5 us (11%)
  waiting for transfers between devices  5.14 us (6%)
  local copies, waits for them, and re-layouts  4.79 us (5%)
  other arithmetic  3.79 us (4%)
    all_to_all x1, blocking collectives, body(): lax.all_to_all(blocks, ('freq', 'grp'), split_axis=0, concat_axis=0, tile...  28.7 us
    pallas_call x1, Pallas kernels, radiate(): pl.pallas_call(radiate_kernel, out_shape=jax.ShapeDtypeStruct((quads // 2...  22.2 us
    pallas_call x1, Pallas kernels, green_start(): pl.pallas_call(prepare_kernel, grid=(panels // size,), out_shape=(jax.Sha...  13.9 us
    all_to_all x1, starting transfers between devices, body(): lax.all_to_all(blocks, 'freq', split_axis=0, concat_axis=0, tiled=True)  10.5 us
    all_to_all x1, waiting for transfers between devices, body(): lax.all_to_all(blocks, 'freq', split_axis=0, concat_axis=0, tiled=True)  5.14 us
    pallas_call x1, Pallas kernels, regroup(): pl.pallas_call(regroup_kernel, out_shape=jax.ShapeDtypeStruct((owners, ro...  3.1 us
    unnamed x12, local copies, waits for them, and re-layouts  2.07 us
    convert_element_type x1, other arithmetic, transform_table(): return rows.astype(BF16).reshape(2 * NF, NT)  2.03 us
  transfers between devices with their start and end apart: 1, of which 1 were waited for; matrix products, arithmetic and copies ran while one was open for 7% of the time, Pallas kernels for 15%

profile of v4, /device:TPU:1, one launch (start us, length us, event | category | flops | bytes accessed | tf_op | source)
XLA Modules:
  0.0 93.0 jit_solution(13555182017647255885)
XLA Ops:
  0.0 0.0 copy-start
  0.0 0.0 copy-start.2
  0.0 3.1 %regroup.1 = bf16[64,16,1024]{2,1,0:T(8,128)(2,1)} custom-call(bf16[16,65536]{1,0:T(8,128)(2,1)} %source_hbm.1), custom_call_target="tpu_custom_call" | custom-call | tf_op jit(solution)/shard_map/regroup/pallas_call | solution.py:352
  3.1 0.0 copy-start.4
  3.1 10.5 %all-to-all-start = ((bf16[64,16,1024]{2,1,0:T(8,128)(2,1)}), bf16[64,16,1024]{2,1,0:T(8,128)(2,1)}, u32[]{:S(2)}, u32[]{:S(2)}) async-start(bf16[64,16,1024]{2,1,0:T(8,128)(2,1)} %regroup.1), calls=%async_computation | async-start | bytes 4194304 | tf_op jit(solution)/shard_map/all_to_all | solution.py:373
  13.7 0.7 dynamic_slice.6
  14.4 0.0 copy-start.3
  14.4 0.6 slice.3
  14.9 0.0 copy-done
  15.0 0.2 copy.17
  15.2 0.3 sine_multiply_fusion
  15.6 1.1 %fusion.3 = (f32[64,1024]{1,0:T(8,128)S(1)}, f32[64,1024]{1,0:T(8,128)S(1)}) fusion(s32[64]{0:T(128)S(1)} %get-tuple-element.22, s32[64]{0:T(128)S(1)} %get-tuple-element.21), kind=kLoop, calls=%fused_computation.9 | loop fusion | flops 983040 | bytes 524800 | tf_op jit(solution)/shard_map/sin | solution.py:35
  16.7 0.0 copy-done.2
  16.7 0.4 copy.13
  17.1 0.0 copy-done.4
  17.1 0.6 gather_fusion
  17.7 0.1 copy.14
  17.7 0.1 tile.10.observer_ref
  18.5 2.0 %subtract_convert_fusion = bf16[16,64,1024]{2,1,0:T(8,128)(2,1)} fusion(f32[64,1024]{1,0:T(8,128)S(1)} %get-tuple-element.14, f32[16,1024]{1,0:T(8,128)S(1)} %get-tuple-element.13, f32[64,1024]{1,0:T(8,128)S(1)} %get-tuple-element.12, f32[16,1024]{1,0:T(8,128)S(1)} %get-tuple-element.11), kind=kLoop, calls=%fused_computation.1 | loop fusion | flops 4194304 | bytes 2752512 | tf_op jit(solution)/shard_map/convert_element_type | solution.py:39
  20.6 13.9 %prepare.1 = (f32[5,1024,128]{2,1,0:T(8,128)S(1)}, bf16[64,1024,256]{2,1,0:T(8,128)(2,1)}) custom-call(f32[1024,3]{1,0:T(8,128)S(1)} %bitcast.8, f32[3,128]{1,0:T(4,128)S(1)} %tile.10.observer_ref), custom_call_target="tpu_custom_call" | custom-call | flops 5000000000 | bytes 36000000 | tf_op jit(solution)/shard_map/prepare/pallas_call | solution.py:85
  34.5 0.0 copy-done.3
  34.5 0.0 copy-start.1
  34.5 1.5 %copy-done.1 = f32[5,1024,128]{2,1,0:T(8,128)} copy-done((f32[5,1024,128]{2,1,0:T(8,128)}, f32[5,1024,128]{2,1,0:T(8,128)S(1)}, u32[]{:S(2)}) %copy-start.1) | copy-done | bytes 2621464
  36.0 5.1 %all-to-all-done = bf16[64,16,1024]{2,1,0:T(8,128)(2,1)} async-done(((bf16[64,16,1024]{2,1,0:T(8,128)(2,1)}), bf16[64,16,1024]{2,1,0:T(8,128)(2,1)}, u32[]{:S(2)}, u32[]{:S(2)}) %all-to-all-start) | async-done | bytes 2097184 | tf_op jit(solution)/shard_map/all_to_all | solution.py:373
  41.1 22.2 %radiate.1 = bf16[64,16,128]{2,1,0:T(8,128)(2,1)} custom-call(s32[1]{0:T(128)S(6)} %min.3.zero_ref, bf16[1024,1024]{1,0:T(8,128)(2,1)} %bitcast.9, bf16[1024,1024]{1,0:T(8,128)(2,1)} %bitcast.1.source_hbm, f32[5,1024,128]{2,1,0:T(8,128)} %copy-done.1, bf16[64,1024,256]{2,1,0:T(8,128)(2,1)} %get-tuple-element.16.early_hbm, s32[1,1024]{1,0:T(1,128)} %bitcast.14), custom_call_target="tpu_custom_call" | custom-call | flops 20000000000 | bytes 8000000 | tf_op jit(solution)/shard_map/radiate/pallas_call | solution.py:302
  63.3 28.7 %all_to_all.10 = bf16[256,4,128]{2,1,0:T(4,128)(2,1)S(1)} all-to-all(bf16[256,4,128]{2,1,0:T(4,128)(2,1)} %bitcast.10), channel_id=1, replica_groups=mesh['grp'=4,'freq'=64] {'freq','grp'}, dimensions={0} | all-to-all | bytes 524288 | tf_op jit(solution)/shard_map/all_to_all | solution.py:381
  92.0 0.3 convert_reduce_fusion
  92.3 0.1 reshape.60
  92.4 0.6 copy.16
  (7 shorter events, 0.0 us)
Async XLA Ops:
  0.0 14.9 %copy-start = (f32[3,65536]{1,0:T(4,128)S(1)}, f32[3,65536]{1,0:T(4,128)}, u32[]{:S(2)}) copy-start(f32[3,65536]{1,0:T(4,128)} %param.6) | copy-start | bytes 2359300
  0.0 16.7 %copy-start.2 = (f32[3,2048]{1,0:T(4,128)S(1)}, f32[3,2048]{1,0:T(4,128)}, u32[]{:S(2)}) copy-start(f32[3,2048]{1,0:T(4,128)} %param.8) | copy-start | bytes 73732
  3.1 13.9 %copy-start.4 = (s32[32]{0:T(128)S(1)}, s32[32]{0:T(128)}, u32[]{:S(2)}) copy-start(s32[32]{0:T(128)} %param.9) | copy-start | bytes 388
  3.1 38.0 %all-to-all-start = ((bf16[64,16,1024]{2,1,0:T(8,128)(2,1)}), bf16[64,16,1024]{2,1,0:T(8,128)(2,1)}, u32[]{:S(2)}, u32[]{:S(2)}) async-start(bf16[64,16,1024]{2,1,0:T(8,128)(2,1)} %regroup.1), calls=%async_computation | async-start | bytes 4194304 | tf_op jit(solution)/shard_map/all_to_all | solution.py:373
  14.4 20.1 %copy-start.3 = (s32[1024]{0:T(1024)}, s32[1024]{0:T(1024)S(1)}, u32[]{:S(2)}) copy-start(s32[1024]{0:T(1024)S(1)} %dynamic_slice.6) | copy-start | bytes 12292
  34.5 1.5 %copy-start.1 = (f32[5,1024,128]{2,1,0:T(8,128)}, f32[5,1024,128]{2,1,0:T(8,128)S(1)}, u32[]{:S(2)}) copy-start(f32[5,1024,128]{2,1,0:T(8,128)S(1)} %get-tuple-element.15.start_ref) | copy-start | bytes 7864324
